TPU v7x, 256 devices: a 8x8x2 block of a 8x8x16 slice. The times are simulated.
256 devices in a mesh: member: 2 (over z), lat: 128 (over x, y, core).
Axes of the slice: x: 8, y: 8, z: 2, core: 2. Of those that a mesh axis runs over, the one named last changes fastest.
The devices are a block of a 8x8x16 slice.
Arguments:
- height: float32 [1024, 32, 1440], P(('member', 'lat')), parts along dimension 0, may hold values from -6 to 6
- zonal_courant: float32 [1024, 32, 1440], P(('member', 'lat')), parts along dimension 0, may hold values from -1.5 to 1.5
- merid_courant: float32 [1024, 32, 1440], P(('member', 'lat')), parts along dimension 0, may hold values from -1.5 to 1.5
- rates: float32 [64], P('member'), parts along dimension 0, may hold values from 0.05 to 0.5
- thresholds: float32 [64], P('member'), parts along dimension 0, may hold values from -3 to 3
- flags: int32 [512], replicated, may hold values from 0 to 1, as said below
- cutoffs: int32 [512], replicated, may hold values from 45 to 360
Outputs:
- filtered_height: float32 [1024, 32, 1440], P(('member', 'lat')), parts along dimension 0
There are 2 independent parts, one for each index of `member`. A program takes and returns all parts, laid end to end along the dimension named above; an argument that names none is the same for every part. Nothing has to cross between parts.
Inputs may be any that keep to these rules, and one draw needn't show every extreme that they name: flags is 1 on a southern band of rows that starts at row 0 and on a northern band that ends at row 511, each band 512 // 8 to 128 rows long, and 0 on all other rows.
All inputs are finite; a program needn't handle non-finite values.
Results may differ from a plain program's by a relative error of at most 0.00007.
Values sent between devices are 32-bit elements; how exact they have to be, the bound alone decides.
A program may use at most 64 MiB of HBM per device.

v0:
```python
import jax
import jax.numpy as jnp
from jax import lax
from jax.sharding import Mesh
from jax.sharding import PartitionSpec as P

LAT = ("lat_0", "lat_1", "lat_2")
MEMBER_LAT = ("member", "lat_0", "lat_1", "lat_2")


def padded_2(cells, sides, width):
    for axis, dim in sides:
        count = lax.axis_size(axis)
        ends = count - 1
        head = lax.slice_in_dim(cells, 0, width, axis=dim)
        tail = lax.slice_in_dim(cells, cells.shape[dim] - width, cells.shape[dim], axis=dim)
        cells = jnp.concatenate(
            [
                lax.ppermute(tail, axis, [(i, (i + 1) % count) for i in range(ends)]),
                cells,
                lax.ppermute(head, axis, [((i + 1) % count, i) for i in range(ends)]),
            ],
            axis=dim,
        )
    return cells


def one_axis_at_a_time(array, axes):
    for axis in axes:
        array = lax.psum(array, axis)
    return array


def transform_table(nlon, nkp):
    points = jnp.arange(nlon, dtype=jnp.int32)
    waves = jnp.arange(nkp, dtype=jnp.int32)
    phase = points[:, None] * waves[None, :] % nlon
    angle = 2.0 * jnp.pi / nlon * phase.astype(jnp.float32)
    return jnp.concatenate([jnp.cos(angle), jnp.sin(angle)], axis=1)


def wave_weights(nlon, nkp):
    waves = jnp.arange(nkp, dtype=jnp.int32)
    interior = jnp.where((waves > 0) & (waves < nlon // 2), 2.0, 1.0)
    return jnp.where(waves <= nlon // 2, interior, 0.0).astype(jnp.float32) / nlon


def damping(row_flags, row_cutoffs, nkp):
    waves = jnp.maximum(jnp.arange(nkp), 1).astype(jnp.float32)
    ratio = row_cutoffs.astype(jnp.float32)[:, None] / waves[None, :]
    factor = jnp.minimum(1.0, ratio * ratio)
    return jnp.where(row_flags[:, None] > 0, factor, 1.0)


def filter_units(flat, damp, table, weights):
    highest = lax.Precision.HIGHEST
    spectrum = jnp.dot(flat, table, precision=highest, preferred_element_type=jnp.float32)
    factor = (1.0 - damp) * weights[None, :]
    scaled = spectrum * jnp.concatenate([factor, factor], axis=1)
    dims = (((1,), (1,)), ((), ()))
    removed = lax.dot_general(
        scaled, table, dims, precision=highest, preferred_element_type=jnp.float32
    )
    return flat - removed


def filtered_or_kept(block, row_flags, row_cutoffs, table, weights):
    rows, levels, nlon = block.shape
    damp = damping(row_flags, row_cutoffs, weights.shape[0])
    unit_damp = jnp.broadcast_to(damp[:, None, :], (rows, levels, damp.shape[1])).reshape(
        rows * levels, damp.shape[1]
    )

    def apply_filter(data):
        return filter_units(data.reshape(rows * levels, nlon), unit_damp, table, weights).reshape(
            rows, levels, nlon
        )

    def keep_block(data):
        return data

    return lax.cond(jnp.any(row_flags > 0), apply_filter, keep_block, block)


def face_fluxes(rows_height, rows_speed, face_cos, count):
    face_value = (
        7.0 * (rows_height[1 : count + 1] + rows_height[2 : count + 2])
        - (rows_height[0:count] + rows_height[3 : count + 3])
    ) / 12.0
    speed = 0.5 * (rows_speed[0:count] + rows_speed[1 : count + 1]) * face_cos[:, None, None]
    return speed * face_value


def face_cosines(face_ids, nlat):
    return jnp.where(
        (face_ids > 0) & (face_ids < nlat),
        jnp.sin(jnp.pi * face_ids.astype(jnp.float32) / nlat),
        jnp.float32(0.0),
    )


def local(height, zonal_courant, merid_courant, rates, thresholds, flags, cutoffs):
    lat_rows, levels, nlon = height.shape
    devices = lax.axis_size(LAT)
    position = lax.axis_index(LAT)
    first_row = position * lat_rows
    nlat = lat_rows * devices
    local_rows = first_row + jnp.arange(lat_rows, dtype=jnp.int32)
    cos_rows = jnp.sin(jnp.pi * (local_rows.astype(jnp.float32) + 0.5) / nlat)
    faces = first_row + jnp.arange(lat_rows + 1, dtype=jnp.int32)
    cos_faces = face_cosines(faces, nlat)
    padded = padded_2(jnp.stack([height, merid_courant]), ((LAT, 1),), 2)
    east = jnp.roll(height, -1, axis=2)
    west = jnp.roll(height, 1, axis=2)
    far_east = jnp.roll(height, -2, axis=2)
    face_height = (7.0 * (height + east) - (west + far_east)) / 12.0
    face_speed = 0.5 * (zonal_courant + jnp.roll(zonal_courant, -1, axis=2))
    zonal_flux = face_speed * face_height
    zonal_div = zonal_flux - jnp.roll(zonal_flux, 1, axis=2)
    source = -rates[None, :, None] * jax.nn.softplus(height - thresholds[None, :, None])
    partial_sums = jnp.sum(jnp.sum(source, axis=2) * cos_rows[:, None], axis=0)
    totals = one_axis_at_a_time(partial_sums, LAT)
    all_rows = jnp.arange(nlat, dtype=jnp.int32)
    area = nlon * jnp.sum(jnp.sin(jnp.pi * (all_rows.astype(jnp.float32) + 0.5) / nlat))
    level_mean = totals / area
    padded_height = padded[0]
    padded_speed = padded[1]
    count = lat_rows + 1
    merid_flux = face_fluxes(padded_height, padded_speed[1:], cos_faces, count)
    merid_div = (merid_flux[1:] - merid_flux[:-1]) / cos_rows[:, None, None]
    updated = height - zonal_div - merid_div + source - level_mean[None, :, None]
    nkp = (nlon // 2 + 128) // 128 * 128
    table = transform_table(nlon, nkp)
    weights = wave_weights(nlon, nkp)
    row_flags = lax.dynamic_slice_in_dim(flags, first_row, lat_rows)
    row_cutoffs = lax.dynamic_slice_in_dim(cutoffs, first_row, lat_rows)
    result = filtered_or_kept(updated, row_flags, row_cutoffs, table, weights)
    return result


def solution(mesh):
    finer = Mesh(
        mesh.devices.reshape(mesh.shape["member"], 8, 8, 2), ("member", "lat_0", "lat_1", "lat_2")
    )
    placed = (
        P(MEMBER_LAT, None, None),
        P(MEMBER_LAT, None, None),
        P(MEMBER_LAT, None, None),
        P("member"),
        P("member"),
        P(),
        P(),
    )
    return jax.shard_map(
        local, mesh=finer, in_specs=placed, out_specs=P(MEMBER_LAT, None, None), check_vma=False
    )
```

profile of v0, /device:TPU:513, one launch (start us, length us, event | category | flops | bytes accessed | tf_op | source)
XLA Modules:
  0.0 114.5 jit_solution(6825483343422072671)
XLA Ops:
  0.0 2.5 %fusion.17 = (f32[2,2,32,1440]{3,2,1,0:T(8,128)}, f32[2,2,32,1440]{3,2,1,0:T(8,128)S(1)}) fusion(f32[1,4,32,1440]{3,2,1,0:T(8,128)} %bitcast.21, f32[1,4,32,1440]{3,2,1,0:T(8,128)} %bitcast.27), kind=kLoop, calls=%fused_computation.33 | loop fusion | flops 368640 | bytes 2949120 | tf_op jit(solution)/shard_map/stack | solution.py:112
  2.5 5.7 %collective-permute-start = (f32[2,2,32,1440]{3,2,1,0:T(8,128)}, f32[2,2,32,1440]{3,2,1,0:T(8,128)}, u32[]{:S(2)}, u32[]{:S(2)}) collective-permute-start(f32[2,2,32,1440]{3,2,1,0:T(8,128)} %get-tuple-element.115), channel_id=1, source_target_pairs={{0,1},{1,2},{2,3},{3,4},{4,5},{5,6},{6,7},{7,8},{8,9},{9,10},{10,1... | collective-permute-start | bytes 2211848 | tf_op jit(solution)/shard_map/ppermute | solution.py:19
  8.2 18.8 %collective-permute-start.1 = (f32[2,2,32,1440]{3,2,1,0:T(8,128)S(1)}, f32[2,2,32,1440]{3,2,1,0:T(8,128)}, u32[]{:S(2)}, u32[]{:S(2)}) collective-permute-start(f32[2,2,32,1440]{3,2,1,0:T(8,128)S(1)} %get-tuple-element.116), channel_id=1, source_target_pairs={{1,0},{2,1},{3,2},{4,3},{5,4},{6,5},{7,6},{8,7},{9,8},{10,9},{11,1... | collective-permute-start | bytes 2211848 | tf_op jit(solution)/shard_map/ppermute | solution.py:21
  27.1 1.6 %fusion.33 = (f32[4,32,1439]{2,1,0:T(8,128)S(1)}, f32[4,32,1439]{2,1,0:T(8,128)S(1)}) fusion(f32[4,32,1440]{2,1,0:T(8,128)} %param.9), kind=kLoop, calls=%fused_computation.63 | loop fusion | bytes 2947072 | tf_op jit(solution)/shard_map/jit(_roll_static)/slice | solution.py:114
  28.8 0.1 fusion.32
  28.9 0.3 slice.95
  29.2 0.3 slice.89
  29.5 0.7 sine_reduce_fusion
  30.2 19.5 %fusion.7 = (f32[1440,768]{1,0:T(8,128)}, f32[1440,768]{1,0:T(8,128)}) fusion(), kind=kLoop, calls=%fused_computation.15 | loop fusion | flops 9953280 | bytes 8847360 | tf_op jit(solution)/shard_map/sin | solution.py:39
  49.8 0.9 fusion.29
  50.7 0.1 multiply_reduce_fusion
  50.8 10.7 %psum.21 = f32[32]{0:T(128)S(1)} all-reduce(f32[32]{0:T(128)S(1)} %multiply_reduce_fusion), channel_id=1, replica_groups=mesh['member'=2,'lat_0'=8,'lat_1'=8,'lat_2'=2] {'lat_0'}, use_global_device_ids=true, to_apply=%region_3.4 | all-reduce | flops 32 | bytes 256 | tf_op jit(solution)/shard_map/psum | solution.py:30
  61.5 10.7 %psum.22 = f32[32]{0:T(128)S(1)} all-reduce(f32[32]{0:T(128)S(1)} %psum.21), channel_id=1, replica_groups=mesh['member'=2,'lat_0'=8,'lat_1'=8,'lat_2'=2] {'lat_1'}, use_global_device_ids=true, to_apply=%region_4.5 | all-reduce | flops 32 | bytes 256 | tf_op jit(solution)/shard_map/psum | solution.py:30
  72.3 8.5 %psum.23 = f32[32]{0:T(128)S(1)} all-reduce(f32[32]{0:T(128)S(1)} %psum.22), channel_id=1, replica_groups=mesh['member'=2,'lat_0'=8,'lat_1'=8,'lat_2'=2] {'lat_2'}, use_global_device_ids=true, to_apply=%region_5.6 | all-reduce | flops 32 | bytes 256 | tf_op jit(solution)/shard_map/psum | solution.py:30
  80.7 0.1 slice.109
  80.8 1.4 %fusion.31 = (pred[]{:T(512)}, pred[4]{0:T(512)(128)(4,1)S(1)}) fusion(s32[512]{0:T(512)} %param.14, s32[]{:T(128)S(6)} %select_n.50), kind=kLoop, calls=%fused_computation.61 | loop fusion | flops 7 | bytes 25 | tf_op jit(solution)/shard_map/reduce_or | solution.py:82
  82.2 0.8 dynamic-slice_convert_fusion
  84.2 0.0 copy-start.3
  84.3 8.2 %pad_maximum_fusion = f32[1440,1536]{1,0:T(8,128)} fusion(f32[1440,768]{1,0:T(8,128)} %get-tuple-element.123, f32[1440,768]{1,0:T(8,128)} %get-tuple-element.124), kind=kLoop, calls=%fused_computation.8 | loop fusion | flops 2211840 | bytes 17694720 | tf_op jit(solution)/shard_map/concatenate | solution.py:39
  92.4 0.0 collective-permute-done
  92.4 0.0 collective-permute-done.1
  92.4 1.9 %maximum_maximum_fusion = (f32[2,6,32,1440]{3,2,1,0:T(8,128)S(1)}, f32[2,6,32,1440]{3,2,1,0:T(8,128)S(1)}) fusion(f32[1,4,32,1440]{3,2,1,0:T(8,128)S(1)} %bitcast.28, f32[1,4,32,1440]{3,2,1,0:T(8,128)S(1)} %bitcast.22, f32[2,2,32,1440]{3,2,1,0:T(8,128)} %collective-permute-done, f32[2,2,32,1440]{3,2,1,0:T(8,128)} %collective-permute-done.1), kind=kLoop, calls=%fused_computation.18 | loop fusion | flops 2211840 | bytes 7372800 | tf_op jit(solution)/shard_map/concatenate | solution.py:17
  94.4 0.5 fusion.13
  94.9 0.7 fusion.22
  95.6 18.0 %conditional.1 = (f32[4,32,1440]{2,1,0:T(8,128)S(1)}) conditional(s32[]{:T(128)} %convert_element_type.42, f32[4,32,1440]{2,1,0:T(8,128)S(1)} %fusion.22, (f32[4,32,1440]{2,1,0:T(8,128)S(1)}, f32[1440,1536]{1,0:T(8,128)}, pred[4]{0:T(512)(128)(4,1)S(1)}, f32[4]{0:T(128)S(1)}, f32[1,768]{1,0:T(1,128)S(1)}, /*index=5*/s32[768]{0:T(1024)S(1)}) %tuple.45), branch_computations={%region_7.8_spmd, %region_8.9_spmd} | conditional | flops 6795468800 | bytes 25258016 | solution.py:82
  95.9 0.1 fusion.2
  96.0 7.6 %convolution_multiply_fusion = f32[128,1536]{1,0:T(8,128)S(1)} fusion(f32[128,1440]{1,0:T(8,128)S(1)} %bitcast.24, f32[1440,1536]{1,0:T(8,128)} %get-tuple-element.105, f32[128,768]{1,0:T(8,128)S(1)} %bitcast_multiply_fusion), kind=kOutput, calls=%fused_computation.1 | convolution fusion | flops 3397779456 | bytes 10764288 | tf_op jit(solution)/shard_map/cond/branch_1_fun/dot_general | solution.py:57
  103.6 0.3 copy.27
  103.9 9.5 %convolution_subtract_fusion = f32[128,1440]{0,1:T(8,128)S(1)} fusion(f32[128,1440]{0,1:T(8,128)S(1)} %copy.27, f32[128,1536]{1,0:T(8,128)S(1)} %convolution_multiply_fusion, f32[1440,1536]{1,0:T(8,128)} %get-tuple-element.105), kind=kOutput, calls=%fused_computation | convolution fusion | flops 3397570560 | bytes 11108352 | tf_op jit(solution)/shard_map/cond/branch_1_fun/dot_general | solution.py:61
  113.4 0.3 copy.28
  113.6 0.0 copy-start.1
  113.7 0.9 copy-done.1
  (21 shorter events, 0.2 us)
Async XLA Ops:
  0.0 28.8 %copy-start = (f32[4,32,1440]{2,1,0:T(8,128)S(1)}, f32[4,32,1440]{2,1,0:T(8,128)}, u32[]{:S(2)}) copy-start(f32[4,32,1440]{2,1,0:T(8,128)} %param.9) | copy-start | bytes 2211844
  0.0 29.2 %copy-start.2 = (f32[4,32,1440]{2,1,0:T(8,128)S(1)}, f32[4,32,1440]{2,1,0:T(8,128)}, u32[]{:S(2)}) copy-start(f32[4,32,1440]{2,1,0:T(8,128)} %param.10) | copy-start | bytes 2211844
  2.5 89.9 %collective-permute-start = (f32[2,2,32,1440]{3,2,1,0:T(8,128)}, f32[2,2,32,1440]{3,2,1,0:T(8,128)}, u32[]{:S(2)}, u32[]{:S(2)}) collective-permute-start(f32[2,2,32,1440]{3,2,1,0:T(8,128)} %get-tuple-element.115), channel_id=1, source_target_pairs={{0,1},{1,2},{2,3},{3,4},{4,5},{5,6},{6,7},{7,8},{8,9},{9,10},{10,1... | collective-permute-start | bytes 2211848 | tf_op jit(solution)/shard_map/ppermute | solution.py:19
  8.2 84.2 %collective-permute-start.1 = (f32[2,2,32,1440]{3,2,1,0:T(8,128)S(1)}, f32[2,2,32,1440]{3,2,1,0:T(8,128)}, u32[]{:S(2)}, u32[]{:S(2)}) collective-permute-start(f32[2,2,32,1440]{3,2,1,0:T(8,128)S(1)} %get-tuple-element.116), channel_id=1, source_target_pairs={{1,0},{2,1},{3,2},{4,3},{5,4},{6,5},{7,6},{8,7},{9,8},{10,9},{11,1... | collective-permute-start | bytes 2211848 | tf_op jit(solution)/shard_map/ppermute | solution.py:21
  30.2 19.5 %copy-start.5 = (f32[32]{0:T(128)S(1)}, f32[32]{0:T(128)}, u32[]{:S(2)}) copy-start(f32[32]{0:T(128)} %param.12) | copy-start | bytes 388
  30.2 19.6 %slice-start = ((f32[4,32,1440]{2,1,0:T(8,128)}), f32[4,32,1]{2,1,0:T(8,128)S(1)}, s32[]{:S(2)}) async-start(f32[4,32,1440]{2,1,0:T(8,128)} %param.10), calls=%async_computation | async-start | bytes 131072 | tf_op jit(solution)/shard_map/jit(_roll_static)/slice | solution.py:117
  30.2 19.6 %copy-start.4 = (f32[32]{0:T(128)S(1)}, f32[32]{0:T(128)}, u32[]{:S(2)}) copy-start(f32[32]{0:T(128)} %param.13) | copy-start | bytes 388
  84.2 8.2 %copy-start.3 = (f32[4,32,1440]{2,1,0:T(8,128)S(1)}, f32[4,32,1440]{2,1,0:T(8,128)}, u32[]{:S(2)}) copy-start(f32[4,32,1440]{2,1,0:T(8,128)} %param.11) | copy-start | bytes 2211844
  113.6 0.9 copy-start.1
where the time goes:
time: 115 us
  other arithmetic  37.4 us (33%)
  blocking collectives  30 us (26%)
  starting transfers between devices  24.5 us (21%)
  matrix products  17.1 us (15%)
  local copies, waits for them, and re-layouts  3.78 us (3%)
  between operations  1.42 us (1%)
    psum x3, blocking collectives, one_axis_at_a_time(): array = lax.psum(array, axis)  30 us
    sin x1, other arithmetic, transform_table(): return jnp.concatenate([jnp.cos(angle), jnp.sin(angle)], axis=1)  19.5 us
    ppermute x1, starting transfers between devices, padded_2(): lax.ppermute(head, axis, [((i + 1) % count, i) for i in range(ends)])  18.8 us
    dot_general x1, matrix products, filter_units(): lax.dot_general(scaled, table, dims, precision=highest, preferred_element...  9.48 us
    concatenate x1, other arithmetic, transform_table(): return jnp.concatenate([jnp.cos(angle), jnp.sin(angle)], axis=1)  8.16 us
    dot_general x1, matrix products, filter_units(): jnp.dot(flat, table, precision=highest, preferred_element_type=jnp.float32)  7.63 us
    ppermute x1, starting transfers between devices, padded_2(): lax.ppermute(tail, axis, [(i, (i + 1) % count) for i in range(ends)])  5.73 us
    another operation x1, other arithmetic, local(): padded = padded_2(jnp.stack([height, merid_courant]), ((LAT, 1),), 2)  2.49 us
  transfers between devices with their start and end apart: 2, of which 0 were waited for; matrix products, arithmetic and copies ran while one was open for 30% of the time, Pallas kernels for 0%

commit v1 on v0

v1 whole, which is shorter than its diff:
```python
import functools
import math

import jax
import jax.numpy as jnp
import numpy as np
from jax import lax
from jax.experimental import pallas as pl
from jax.experimental.pallas import tpu as pltpu
from jax.sharding import Mesh
from jax.sharding import PartitionSpec as P

MESH = pl.DeviceIdType.MESH
NX, NY, NC = 8, 8, 2
RADIX = 12
HALF = 128
ROOT = math.sqrt(0.75)


def filter_tables(nlon):
    count = nlon // RADIX
    tiles = RADIX // 2
    fwd = np.zeros((tiles, 2 * HALF, 2 * HALF))
    inv = np.zeros((tiles, 2 * HALF, 2 * HALF))
    waves = np.zeros((8, 2 * HALF), np.int64)
    r = np.arange(count)

    def trig(k):
        angle = 2.0 * np.pi / nlon * ((r * k) % nlon)
        return np.cos(angle), np.sin(angle)

    def real_part(base, shift):
        lane = base
        for q in range(count // 2 + 1):
            k = RADIX * q + shift
            if k > nlon // 2:
                continue
            cos, sin = trig(k)
            weight = (1.0 if k in (0, nlon // 2) else 2.0) / nlon
            rows = slice(base, base + count)
            fwd[0, rows, lane] = cos
            inv[0, lane, rows] = cos * weight
            waves[0, lane] = k
            lane += 1
            if k not in (0, nlon // 2):
                fwd[0, rows, lane] = sin
                inv[0, lane, rows] = sin * weight
                waves[0, lane] = k
                lane += 1
        assert lane == base + count

    real_part(0, 0)
    real_part(HALF, RADIX // 2)
    for m in range(1, tiles):
        for q in range(count):
            k = RADIX * q + m
            cos, sin = trig(k)
            fwd[m, 0:count, q] = cos
            fwd[m, HALF : HALF + count, q] = -sin
            fwd[m, 0:count, HALF + q] = sin
            fwd[m, HALF : HALF + count, HALF + q] = cos
            waves[m, q] = waves[m, HALF + q] = min(k, nlon - k)
        inv[m] = fwd[m].T * (2.0 / nlon)
    inv_square = 1.0 / np.maximum(waves, 1).astype(np.float64) ** 2

    def halves(table):
        hi = table.astype(np.float32).astype(jnp.bfloat16)
        lo = (table - hi.astype(np.float64)).astype(np.float32).astype(jnp.bfloat16)
        return np.stack([hi, lo])

    return halves(fwd), halves(inv), inv_square.astype(np.float32)


def row_scalars(nlat):
    rows = np.arange(nlat)
    cos_row = np.sin(np.pi * (rows + 0.5) / nlat)
    faces = np.arange(nlat + 1)
    cos_face = np.where((faces > 0) & (faces < nlat), np.sin(np.pi * faces / nlat), 0.0)
    table = np.zeros((3 * nlat + HALF,))
    table[0:nlat] = cos_row
    table[nlat : 2 * nlat] = 1.0 / cos_row
    table[2 * nlat : 3 * nlat + 1] = cos_face / 24.0
    return table.astype(np.float32), float(np.sum(cos_row))


def twelve(e, o):
    plus, minus = e[0] + e[6], e[0] - e[6]
    e15p, e15m, e24p, e24m = e[1] + e[5], e[1] - e[5], e[2] + e[4], e[2] - e[4]
    a, b = plus + e24p, e15p + e[3]
    big, mid = ROOT * e15m, minus + 0.5 * e24m
    c, d = plus - 0.5 * e24p, 0.5 * e15p - e[3]
    even = [a + b, mid + big, c + d, minus - e24m, c - d, mid - big, a - b]
    o15p, o15m, o24p, o24m = o[0] + o[4], o[0] - o[4], o[1] + o[3], o[1] - o[3]
    f, g = 0.5 * o15p + o[2], ROOT * o24p
    s, t = ROOT * o15m, ROOT * o24m
    odd = [f + g, s + t, o15p - o[2], s - t, f - g]
    return even, odd


def split(x):
    hi = x.astype(jnp.bfloat16)
    return hi, (x - hi.astype(jnp.float32)).astype(jnp.bfloat16)


def kernel(
    dims, area, chunks,
    h_hbm, z_hbm, c_hbm, rates_hbm, thr_hbm, flags_hbm, cut_hbm, scal_hbm, ksq_hbm, fwd_hbm, inv_hbm,
    out,
    h, z, c, rates, thr, flags, cut, scal, ksq, fwd, inv,
    halo_h, halo_c, base, s_lo, s_hi, factor, ymat, wmat, part, xbuf, ysum, ybuf,
    in_sem, halo_send, halo_recv, x_send, x_recv, y_send, y_recv,
):
    rows, levels, nlon, nlat = dims
    count = nlon // RADIX
    x, y, core = lax.axis_index("lat_0"), lax.axis_index("lat_1"), lax.axis_index("lat_2")
    position = (x * NY + y) * NC + core
    total = NX * NY * NC

    local = [
        pltpu.make_async_copy(src, dst, in_sem.at[i])
        for i, (src, dst) in enumerate(
            [
                (h_hbm, h), (c_hbm, c), (rates_hbm, rates), (thr_hbm, thr), (scal_hbm, scal), (z_hbm, z),
                (flags_hbm, flags), (cut_hbm, cut), (ksq_hbm, ksq), (fwd_hbm, fwd), (inv_hbm, inv),
            ]
        )
    ]
    for copy in local:
        copy.start()

    def along(step):
        p = lax.rem(position + total + step, total)
        return {"lat_0": p // (NY * NC), "lat_1": lax.rem(p // NC, NY), "lat_2": lax.rem(p, NC)}

    def at_x(dx, k):
        return {"lat_0": lax.rem(x + dx, NX), "lat_1": y, "lat_2": k}

    def at_y(dy, k):
        return {"lat_0": x, "lat_1": lax.rem(y + dy + NY, NY), "lat_2": k}

    barrier = pltpu.get_barrier_semaphore()
    peers = [along(1), along(-1), at_x(0, 1 - core)]
    for k in range(NC):
        peers += [at_x(d, k) for d in range(1, NX)] + [at_y(d, k) for d in range(1, NY)]
    for peer in peers:
        pl.semaphore_signal(barrier, inc=1, device_id=peer, device_id_type=MESH)
    ymat[...] = jnp.zeros_like(ymat)
    pl.semaphore_wait(barrier, len(peers))

    local[0].wait()
    local[1].wait()
    halos = []
    for i, (start, size) in enumerate(chunks):
        lev = pl.ds(start, size)
        group = []
        for side, step, h_rows, c_row in ((0, 1, rows - 2, rows - 1), (1, -1, 0, 0)):
            group.append(
                pltpu.make_async_remote_copy(
                    h.at[pl.ds(h_rows, 2), lev], halo_h.at[side, :, lev],
                    halo_send.at[i, side, 0], halo_recv.at[i, side, 0], device_id=along(step), device_id_type=MESH,
                )
            )
            group.append(
                pltpu.make_async_remote_copy(
                    c.at[c_row, lev], halo_c.at[side, lev],
                    halo_send.at[i, side, 1], halo_recv.at[i, side, 1], device_id=along(step), device_id_type=MESH,
                )
            )
        for copy in group:
            copy.start()
        halos.append(group)

    for i in (2, 3, 4):
        local[i].wait()
    first = position * rows

    lane = lax.broadcasted_iota(jnp.int32, (8, HALF), 1)
    tile = jnp.zeros((8, HALF), jnp.float32)
    sub = lax.broadcasted_iota(jnp.int32, (8, 1), 0)

    def column(ref, start):
        value = jnp.zeros((8, 1), jnp.float32)
        for k in range(8):
            value = jnp.where(sub == k, ref[start + k], value)
        return value

    for g in range(levels // 8):
        lev = pl.ds(8 * g, 8)
        rate, threshold = column(rates, 8 * g), column(thr, 8 * g)
        sums = jnp.zeros((8, 1), jnp.float32)
        for r in range(rows):
            height = h[r, lev, :]
            s = height - threshold
            source = -rate * (jnp.maximum(s, 0.0) + jnp.log(1.0 + jnp.exp(-jnp.abs(s))))
            base[r, lev, :] = height + source
            sums = sums + scal[first + r] * jnp.sum(source, axis=1, keepdims=True)
        tile = jnp.where(lane == g, sums, tile)
    part[...] = tile

    x_out = [
        pltpu.make_async_remote_copy(
            part, xbuf.at[core], x_send.at[0], x_recv.at[core], device_id=at_x(0, 1 - core), device_id_type=MESH
        )
    ]
    for d in range(1, NX):
        for k in range(NC):
            x_out.append(
                pltpu.make_async_remote_copy(
                    part, xbuf.at[(NX - d) * NC + core], x_send.at[d * NC + k], x_recv.at[(NX - d) * NC + core],
                    device_id=at_x(d, k), device_id_type=MESH,
                )
            )
    for copy in x_out:
        copy.start()

    local[5].wait()

    def inv_cos(r):
        return scal[nlat + first + r]

    def face(f):
        return scal[2 * nlat + first + f]

    def west(a):
        return pltpu.roll(a, 1, axis=1)

    def east(a):
        return pltpu.roll(a, nlon - 1, axis=1)

    def local_terms(g, carry):
        lev = pl.ds(pl.multiple_of(8 * g, 8), 8)
        hr = [h[r, lev, :] for r in range(rows)]
        cr = [c[r, lev, :] for r in range(rows)]
        low = face(1) * (cr[0] + cr[1])
        high = face(3) * (cr[2] + cr[3])
        s_lo[lev, :] = low
        s_hi[lev, :] = high
        f1 = low * (7.0 * (hr[0] + hr[1]) - hr[2])
        f2 = face(2) * (cr[1] + cr[2]) * (7.0 * (hr[1] + hr[2]) - (hr[0] + hr[3]))
        f3 = high * (7.0 * (hr[2] + hr[3]) - hr[1])
        terms = [f1, f2 - f1, f3 - f2, -f3]
        for r in range(rows):
            pair = hr[r] + east(hr[r])
            zr = z[r, lev, :]
            speed = zr + east(zr)
            flux = speed * (8.0 * pair - (west(pair) + east(pair))) * (1.0 / 24.0)
            base[r, lev, :] = base[r, lev, :] - (flux - west(flux)) - terms[r] * inv_cos(r)
        return carry

    lax.fori_loop(0, levels // 8, local_terms, 0)

    for i in (6, 7, 8):
        local[i].wait()
    for r in range(rows):
        cutoff = cut[first + r].astype(jnp.float32)
        flag = flags[first + r].astype(jnp.float32)
        factor[r] = flag * (1.0 - jnp.minimum(1.0, cutoff * cutoff * ksq[...]))

    def landed(ref, sem):
        pltpu.make_async_copy(ref, ref, sem).wait()

    landed(xbuf.at[1 - core], x_recv.at[1 - core])
    total_x = part[...] + xbuf[1 - core]
    for slot in range(NC, NX * NC):
        landed(xbuf.at[slot], x_recv.at[slot])
        total_x = total_x + xbuf[slot]
    ysum[...] = total_x
    sign = 1 - 2 * core
    y_out = []
    for d in range(1, 4):
        for k in range(NC):
            y_out.append(
                pltpu.make_async_remote_copy(
                    ysum, ybuf.at[3 * core + d - 1], y_send.at[2 * d - 2 + k], y_recv.at[3 * core + d - 1],
                    device_id=at_y(sign * d, k), device_id_type=MESH,
                )
            )
    y_out.append(
        pltpu.make_async_remote_copy(
            ysum, ybuf.at[6], y_send.at[6], y_recv.at[6], device_id=at_y(4, core), device_id_type=MESH
        )
    )
    for copy in y_out:
        copy.start()

    local[9].wait()
    local[10].wait()
    keep_lo = jnp.where(position > 0, 1.0, 0.0)
    keep_hi = jnp.where(position < total - 1, 1.0, 0.0)
    for i, (start, size) in enumerate(chunks):
        for copy in halos[i]:
            copy.wait_recv()

        def edges(g, carry):
            lev = pl.ds(pl.multiple_of(start + 8 * g, 8), 8)
            h0, h1, h2, h3 = (h[r, lev, :] for r in range(rows))
            below, below2 = halo_h[0, 1, lev, :], halo_h[0, 0, lev, :]
            above, above2 = halo_h[1, 0, lev, :], halo_h[1, 1, lev, :]
            t1 = keep_lo * (s_lo[lev, :] * below)
            t3 = keep_hi * (s_hi[lev, :] * above)
            f0 = face(0) * (halo_c[0, lev, :] + c[0, lev, :]) * (7.0 * (below + h0) - (below2 + h1))
            f4 = face(4) * (halo_c[1, lev, :] + c[3, lev, :]) * (7.0 * (above + h3) - (above2 + h2))
            base[0, lev, :] = base[0, lev, :] + (t1 + f0) * inv_cos(0)
            base[1, lev, :] = base[1, lev, :] - t1 * inv_cos(1)
            base[2, lev, :] = base[2, lev, :] + t3 * inv_cos(2)
            base[3, lev, :] = base[3, lev, :] - (t3 + f4) * inv_cos(3)
            return carry

        lax.fori_loop(0, size // 8, edges, 0)

        blocks = size // 16
        units = rows * size

        def block_of(b):
            r = b // blocks
            lev = pl.ds(pl.multiple_of(start + 16 * lax.rem(b, blocks), 16), 16)
            return r, lev, pl.ds(pl.multiple_of(16 * b, 16), 16), pl.ds(pl.multiple_of(units + 16 * b, 16), 16)

        def forward(b, carry):
            r, lev, at_hi, at_lo = block_of(b)
            u = [base[r, lev, count * j : count * (j + 1)] for j in range(RADIX)]
            e = [u[0]] + [u[j] + u[RADIX - j] for j in range(1, 6)] + [u[6]]
            o = [u[j] - u[RADIX - j] for j in range(1, 6)]
            even, odd = twelve(e, o)
            halves = [(even[0], even[6])] + [(even[m], odd[m - 1]) for m in range(1, 6)]
            for m, pair in enumerate(halves):
                for k, value in enumerate(pair):
                    hi, lo = split(value)
                    ymat[m, at_hi, HALF * k : HALF * k + count] = hi
                    ymat[m, at_lo, HALF * k : HALF * k + count] = lo
            return carry

        lax.fori_loop(0, rows * blocks, forward, 0)

        def product(hilo, table):
            first_part = jnp.dot(hilo, table[0], preferred_element_type=jnp.float32)
            second = jnp.dot(hilo[0:units], table[1], preferred_element_type=jnp.float32)
            return first_part[0:units] + first_part[units : 2 * units] + second

        for m in range(RADIX // 2):
            waves = product(ymat[m, 0 : 2 * units, :], (fwd[0, m], fwd[1, m]))
            scaled = jnp.concatenate(
                [waves[r * size : (r + 1) * size] * factor[r, m : m + 1, :] for r in range(rows)], axis=0
            )
            wmat[m, 0:units, :] = product(jnp.concatenate(split(scaled), axis=0), (inv[0, m], inv[1, m]))

        def backward(b, carry):
            r, lev, at, _ = block_of(b)
            w = [[wmat[m, at, HALF * k : HALF * k + count] for k in range(2)] for m in range(RADIX // 2)]
            even, odd = twelve([w[0][0]] + [w[m][0] for m in range(1, 6)] + [w[0][1]], [w[m][1] for m in range(1, 6)])
            removed = [even[0]] + [even[j] + odd[j - 1] for j in range(1, 6)] + [even[6]]
            removed += [even[RADIX - j] - odd[RADIX - j - 1] for j in range(7, RADIX)]
            for j in range(RADIX):
                cols = slice(count * j, count * (j + 1))
                out[r, lev, cols] = base[r, lev, cols] - removed[j]
            return carry

        lax.fori_loop(0, rows * blocks, backward, 0)

    mean = ysum[...]
    for slot in range(7):
        landed(ybuf.at[slot], y_recv.at[slot])
        mean = mean + ybuf[slot]
    mean = mean * (1.0 / area)
    for g in range(levels // 8):
        lev = pl.ds(8 * g, 8)
        shift = jnp.sum(jnp.where(lane == g, mean, 0.0), axis=1, keepdims=True)
        for r in range(rows):
            out[r, lev, :] = out[r, lev, :] - shift

    for group in halos:
        for copy in group:
            copy.wait_send()
    for copy in x_out + y_out:
        copy.wait_send()


def local(height, zonal, merid, rates, thresholds, flags, cutoffs):
    rows, levels, nlon = height.shape
    nlat = rows * NX * NY * NC
    fwd, inv, ksq = filter_tables(nlon)
    scalars, cos_sum = row_scalars(nlat)
    chunks = ((0, levels // 2), (levels // 2, levels // 2))
    most = rows * max(size for _, size in chunks)
    tiles = RADIX // 2
    dims = (rows, levels, nlon, nlat)
    f32, bf16 = jnp.float32, jnp.bfloat16
    vmem, smem, dma = pltpu.VMEM, pltpu.SMEM, pltpu.SemaphoreType.DMA
    operands = (height, zonal, merid, rates, thresholds, flags, cutoffs, scalars, ksq, fwd, inv)
    return pl.pallas_call(
        functools.partial(kernel, dims, nlon * cos_sum, chunks),
        out_shape=jax.ShapeDtypeStruct(height.shape, f32),
        in_specs=[pl.BlockSpec(memory_space=pl.ANY)] * len(operands),
        out_specs=pl.BlockSpec(memory_space=vmem),
        scratch_shapes=[
            vmem(height.shape, f32), vmem(height.shape, f32), vmem(height.shape, f32),
            smem(rates.shape, f32), smem(thresholds.shape, f32), smem(flags.shape, jnp.int32),
            smem(cutoffs.shape, jnp.int32), smem(scalars.shape, f32),
            vmem(ksq.shape, f32), vmem(fwd.shape, bf16), vmem(inv.shape, bf16),
            vmem((2, 2, levels, nlon), f32), vmem((2, levels, nlon), f32), vmem(height.shape, f32),
            vmem((levels, nlon), f32), vmem((levels, nlon), f32), vmem((rows, 8, 2 * HALF), f32),
            vmem((tiles, 2 * most, 2 * HALF), bf16), vmem((tiles, most, 2 * HALF), f32),
            vmem((8, HALF), f32), vmem((NX * NC, 8, HALF), f32), vmem((8, HALF), f32), vmem((7, 8, HALF), f32),
            dma((11,)), dma((len(chunks), 2, 2)), dma((len(chunks), 2, 2)),
            dma((NX * NC,)), dma((NX * NC,)), dma((7,)), dma((7,)),
        ],
        compiler_params=pltpu.CompilerParams(collective_id=0, has_side_effects=True),
        name="advect_filter",
    )(*operands)


def solution(mesh):
    finer = Mesh(
        mesh.devices.reshape(mesh.shape["member"], NX, NY, NC), ("member", "lat_0", "lat_1", "lat_2")
    )
    whole = P(("member", "lat_0", "lat_1", "lat_2"), None, None)
    placed = (whole, whole, whole, P("member"), P("member"), P(), P())
    return jax.shard_map(local, mesh=finer, in_specs=placed, out_specs=whole, check_vma=False)
```

time: 115 us -> 42.6 us (0.37)
  the two profiles are of different devices: /device:TPU:513 before, /device:TPU:515 now
where the time goes in v1:
time: 42.6 us; the launch traced here: 42.5 us
  Pallas kernels  40.4 us (95%)
  local copies, waits for them, and re-layouts  2.07 us (5%)
    pallas_call x1, Pallas kernels, local(): pl.pallas_call(functools.partial(kernel, dims, nlon * cos_sum, chunks), o...  40.4 us
    unnamed x1, local copies, waits for them, and re-layouts  2.07 us

profile of v1, /device:TPU:515, one launch (start us, length us, event | category | flops | bytes accessed | tf_op | source)
XLA Modules:
  0.0 42.5 jit_solution(4914170136856699511)
XLA Ops:
  0.0 40.4 %advect_filter.1 = f32[4,32,1440]{2,1,0:T(8,128)} custom-call(f32[4,32,1440]{2,1,0:T(8,128)} %h_hbm.1, f32[4,32,1440]{2,1,0:T(8,128)} %z_hbm.1, f32[4,32,1440]{2,1,0:T(8,128)} %c_hbm.1, f32[32]{0:T(128)} %rates_hbm.1, f32[32]{0:T(128)} %thr_hbm.1, s32[512]{0:T(512)} %flags_hbm.1, s32[512]{0:T(512)} %cut_hbm.1, f32[1664]{0:T(1024)} %constant.8.clone.scal_hbm, ...), custom_call_target="tpu_custom_call" | custom-call | tf_op jit(solution)/shard_map/advect_filter/pallas_call | solution.py:390
  40.4 2.1 %copy.13 = f32[4,32,1440]{2,1,0:T(8,128)} copy(f32[4,32,1440]{2,1,0:T(8,128)} %advect_filter.1) | data formatting | bytes 1474560

commit v2 on v1

--- a/solution.py
+++ b/solution.py
@@ -108,7 +108,8 @@
     out,
     h, z, c, rates, thr, flags, cut, scal, ksq, fwd, inv,
     halo_h, halo_c, base, s_lo, s_hi, factor, ymat, wmat, part, xbuf, ysum, ybuf,
-    in_sem, halo_send, halo_recv, x_send, x_recv, y_send, y_recv,
+    mean, mean_in,
+    in_sem, halo_send, halo_recv, x_send, x_recv, y_send, y_recv, mean_send, mean_recv, low_in, root_in,
 ):
     rows, levels, nlon, nlat = dims
     count = nlon // RADIX
@@ -128,47 +129,86 @@
     for copy in local:
         copy.start()
 
+    last = NX * NY * NC - 1
+    is_root = jnp.logical_and(x == 0, core == 1)
+
     def along(step):
         p = lax.rem(position + total + step, total)
         return {"lat_0": p // (NY * NC), "lat_1": lax.rem(p // NC, NY), "lat_2": lax.rem(p, NC)}
 
-    def at_x(dx, k):
-        return {"lat_0": lax.rem(x + dx, NX), "lat_1": y, "lat_2": k}
-
-    def at_y(dy, k):
-        return {"lat_0": x, "lat_1": lax.rem(y + dy + NY, NY), "lat_2": k}
+    def row(k):
+        return {"lat_0": jnp.int32(k // NC), "lat_1": y, "lat_2": jnp.int32(k % NC)}
+
+    def column(d):
+        return {"lat_0": jnp.int32(0), "lat_1": y + d, "lat_2": jnp.int32(1)}
+
+    def signal(sem, device):
+        pl.semaphore_signal(sem, inc=1, device_id=device, device_id_type=MESH)
 
     barrier = pltpu.get_barrier_semaphore()
-    peers = [along(1), along(-1), at_x(0, 1 - core)]
-    for k in range(NC):
-        peers += [at_x(d, k) for d in range(1, NX)] + [at_y(d, k) for d in range(1, NY)]
-    for peer in peers:
-        pl.semaphore_signal(barrier, inc=1, device_id=peer, device_id_type=MESH)
-    ymat[...] = jnp.zeros_like(ymat)
-    pl.semaphore_wait(barrier, len(peers))
+
+    @pl.when(position > 0)
+    def _():
+        signal(barrier, along(-1))
+
+    @pl.when(is_root)
+    def _():
+        for k in range(NX * NC):
+            if k != 1:
+                signal(barrier, row(k))
+        for d in range(1, NY):
+
+            @pl.when(y >= d)
+            def _():
+                signal(barrier, column(-d))
+
+    pl.semaphore_wait(barrier, jnp.where(position < last, 1, 0) + jnp.where(is_root, NY - 1 - y, 1))
+
+    @pl.when(position < last)
+    def _():
+        signal(low_in, along(1))
+
+    @pl.when(is_root)
+    def _():
+        for d in range(1, NY):
+
+            @pl.when(y + d < NY)
+            def _():
+                signal(root_in.at[d - 1], column(d))
 
     local[0].wait()
     local[1].wait()
-    halos = []
-    for i, (start, size) in enumerate(chunks):
+
+    def halo_copies(i, side):
+        start, size = chunks[i]
         lev = pl.ds(start, size)
-        group = []
-        for side, step, h_rows, c_row in ((0, 1, rows - 2, rows - 1), (1, -1, 0, 0)):
-            group.append(
-                pltpu.make_async_remote_copy(
-                    h.at[pl.ds(h_rows, 2), lev], halo_h.at[side, :, lev],
-                    halo_send.at[i, side, 0], halo_recv.at[i, side, 0], device_id=along(step), device_id_type=MESH,
-                )
+        step, h_row, c_row = ((1, rows - 2, rows - 1), (-1, 0, 0))[side]
+        sems = [(halo_send.at[i, side, k], halo_recv.at[i, side, k]) for k in range(2)]
+        pairs = ((h.at[pl.ds(h_row, 2), lev], halo_h.at[side, :, lev]), (c.at[c_row, lev], halo_c.at[side, lev]))
+        return [
+            pltpu.make_async_remote_copy(
+                src, dst, send, recv, device_id=along(step), device_id_type=MESH
             )
-            group.append(
-                pltpu.make_async_remote_copy(
-                    c.at[c_row, lev], halo_c.at[side, lev],
-                    halo_send.at[i, side, 1], halo_recv.at[i, side, 1], device_id=along(step), device_id_type=MESH,
-                )
-            )
-        for copy in group:
-            copy.start()
-        halos.append(group)
+            for (src, dst), (send, recv) in zip(pairs, sems)
+        ]
+
+    @pl.when(position < last)
+    def _():
+        for i in range(len(chunks)):
+            for copy in halo_copies(i, 0):
+                copy.start()
+
+    ymat[...] = jnp.zeros_like(ymat)
+
+    @pl.when(position == 0)
+    def _():
+        halo_h[0] = jnp.zeros_like(halo_h[0])
+        halo_c[0] = jnp.zeros_like(halo_c[0])
+
+    @pl.when(position == last)
+    def _():
+        halo_h[1] = jnp.zeros_like(halo_h[1])
+        halo_c[1] = jnp.zeros_like(halo_c[1])
 
     for i in (2, 3, 4):
         local[i].wait()
@@ -178,7 +218,7 @@
     tile = jnp.zeros((8, HALF), jnp.float32)
     sub = lax.broadcasted_iota(jnp.int32, (8, 1), 0)
 
-    def column(ref, start):
+    def levels_of(ref, start):
         value = jnp.zeros((8, 1), jnp.float32)
         for k in range(8):
             value = jnp.where(sub == k, ref[start + k], value)
@@ -186,7 +226,7 @@
 
     for g in range(levels // 8):
         lev = pl.ds(8 * g, 8)
-        rate, threshold = column(rates, 8 * g), column(thr, 8 * g)
+        rate, threshold = levels_of(rates, 8 * g), levels_of(thr, 8 * g)
         sums = jnp.zeros((8, 1), jnp.float32)
         for r in range(rows):
             height = h[r, lev, :]
@@ -197,21 +237,21 @@
         tile = jnp.where(lane == g, sums, tile)
     part[...] = tile
 
-    x_out = [
-        pltpu.make_async_remote_copy(
-            part, xbuf.at[core], x_send.at[0], x_recv.at[core], device_id=at_x(0, 1 - core), device_id_type=MESH
+    def part_copy(slot):
+        return pltpu.make_async_remote_copy(
+            part, xbuf.at[slot], x_send, x_recv.at[slot], device_id=row(1), device_id_type=MESH
         )
-    ]
-    for d in range(1, NX):
-        for k in range(NC):
-            x_out.append(
-                pltpu.make_async_remote_copy(
-                    part, xbuf.at[(NX - d) * NC + core], x_send.at[d * NC + k], x_recv.at[(NX - d) * NC + core],
-                    device_id=at_x(d, k), device_id_type=MESH,
-                )
-            )
-    for copy in x_out:
-        copy.start()
+
+    @pl.when(jnp.logical_not(is_root))
+    def _():
+        part_copy(x * NC + core).start()
+
+    @pl.when(position > 0)
+    def _():
+        pl.semaphore_wait(low_in, 1)
+        for i in range(len(chunks)):
+            for copy in halo_copies(i, 1):
+                copy.start()
 
     local[5].wait()
 
@@ -259,45 +299,71 @@
     def landed(ref, sem):
         pltpu.make_async_copy(ref, ref, sem).wait()
 
-    landed(xbuf.at[1 - core], x_recv.at[1 - core])
-    total_x = part[...] + xbuf[1 - core]
-    for slot in range(NC, NX * NC):
-        landed(xbuf.at[slot], x_recv.at[slot])
-        total_x = total_x + xbuf[slot]
-    ysum[...] = total_x
-    sign = 1 - 2 * core
-    y_out = []
-    for d in range(1, 4):
-        for k in range(NC):
-            y_out.append(
-                pltpu.make_async_remote_copy(
-                    ysum, ybuf.at[3 * core + d - 1], y_send.at[2 * d - 2 + k], y_recv.at[3 * core + d - 1],
-                    device_id=at_y(sign * d, k), device_id_type=MESH,
-                )
-            )
-    y_out.append(
-        pltpu.make_async_remote_copy(
-            ysum, ybuf.at[6], y_send.at[6], y_recv.at[6], device_id=at_y(4, core), device_id_type=MESH
+    def sum_copy(d):
+        return pltpu.make_async_remote_copy(
+            ysum, ybuf.at[y], y_send.at[y + d], y_recv.at[y], device_id=column(d), device_id_type=MESH
         )
-    )
-    for copy in y_out:
-        copy.start()
+
+    def mean_copy(k):
+        return pltpu.make_async_remote_copy(
+            mean, mean_in, mean_send.at[k], mean_recv, device_id=row(k), device_id_type=MESH
+        )
+
+    @pl.when(is_root)
+    def _():
+        acc = part[...]
+        for k in range(NX * NC):
+            if k != 1:
+                landed(xbuf.at[k], x_recv.at[k])
+                acc = acc + xbuf[k]
+        ysum[...] = acc
+        for d in range(1, NY):
+
+            @pl.when(y + d < NY)
+            def _():
+                sum_copy(d).start()
+
+        for d in range(1, NY):
+
+            @pl.when(y >= d)
+            def _():
+                pl.semaphore_wait(root_in.at[d - 1], 1)
+                sum_copy(-d).start()
+
+        mean[...] = acc
+        for k in range(NY):
+
+            @pl.when(y != k)
+            def _():
+                landed(ybuf.at[k], y_recv.at[k])
+                mean[...] = mean[...] + ybuf[k]
+
+        mean[...] = mean[...] * (1.0 / area)
+        for k in range(NX * NC):
+            if k != 1:
+                mean_copy(k).start()
+        mean_in[...] = mean[...]
 
     local[9].wait()
     local[10].wait()
-    keep_lo = jnp.where(position > 0, 1.0, 0.0)
-    keep_hi = jnp.where(position < total - 1, 1.0, 0.0)
     for i, (start, size) in enumerate(chunks):
-        for copy in halos[i]:
-            copy.wait_recv()
+        @pl.when(position > 0)
+        def _():
+            for copy in halo_copies(i, 0):
+                copy.wait_recv()
+
+        @pl.when(position < last)
+        def _():
+            for copy in halo_copies(i, 1):
+                copy.wait_recv()
 
         def edges(g, carry):
             lev = pl.ds(pl.multiple_of(start + 8 * g, 8), 8)
             h0, h1, h2, h3 = (h[r, lev, :] for r in range(rows))
             below, below2 = halo_h[0, 1, lev, :], halo_h[0, 0, lev, :]
             above, above2 = halo_h[1, 0, lev, :], halo_h[1, 1, lev, :]
-            t1 = keep_lo * (s_lo[lev, :] * below)
-            t3 = keep_hi * (s_hi[lev, :] * above)
+            t1 = s_lo[lev, :] * below
+            t3 = s_hi[lev, :] * above
             f0 = face(0) * (halo_c[0, lev, :] + c[0, lev, :]) * (7.0 * (below + h0) - (below2 + h1))
             f4 = face(4) * (halo_c[1, lev, :] + c[3, lev, :]) * (7.0 * (above + h3) - (above2 + h2))
             base[0, lev, :] = base[0, lev, :] + (t1 + f0) * inv_cos(0)
@@ -357,22 +423,40 @@
 
         lax.fori_loop(0, rows * blocks, backward, 0)
 
-    mean = ysum[...]
-    for slot in range(7):
-        landed(ybuf.at[slot], y_recv.at[slot])
-        mean = mean + ybuf[slot]
-    mean = mean * (1.0 / area)
+    @pl.when(jnp.logical_not(is_root))
+    def _():
+        mean_copy(0).wait_recv()
+
     for g in range(levels // 8):
         lev = pl.ds(8 * g, 8)
-        shift = jnp.sum(jnp.where(lane == g, mean, 0.0), axis=1, keepdims=True)
+        shift = jnp.sum(jnp.where(lane == g, mean_in[...], 0.0), axis=1, keepdims=True)
         for r in range(rows):
             out[r, lev, :] = out[r, lev, :] - shift
 
-    for group in halos:
-        for copy in group:
-            copy.wait_send()
-    for copy in x_out + y_out:
-        copy.wait_send()
+    for side, sender in ((0, position < last), (1, position > 0)):
+
+        @pl.when(sender)
+        def _():
+            for i in range(len(chunks)):
+                for copy in halo_copies(i, side):
+                    copy.wait_send()
+
+    @pl.when(is_root)
+    def _():
+        for d in range(1, NY):
+            for step, used in ((d, y + d < NY), (-d, y >= d)):
+
+                @pl.when(used)
+                def _():
+                    sum_copy(step).wait_send()
+
+        for k in range(NX * NC):
+            if k != 1:
+                mean_copy(k).wait_send()
+
+    @pl.when(jnp.logical_not(is_root))
+    def _():
+        part_copy(x * NC + core).wait_send()
 
 
 def local(height, zonal, merid, rates, thresholds, flags, cutoffs):
@@ -387,10 +471,11 @@
     f32, bf16 = jnp.float32, jnp.bfloat16
     vmem, smem, dma = pltpu.VMEM, pltpu.SMEM, pltpu.SemaphoreType.DMA
     operands = (height, zonal, merid, rates, thresholds, flags, cutoffs, scalars, ksq, fwd, inv)
+    operands = [pltpu.with_memory_space_constraint(jnp.asarray(a), pltpu.HBM) for a in operands]
     return pl.pallas_call(
         functools.partial(kernel, dims, nlon * cos_sum, chunks),
-        out_shape=jax.ShapeDtypeStruct(height.shape, f32),
-        in_specs=[pl.BlockSpec(memory_space=pl.ANY)] * len(operands),
+        out_shape=vmem(height.shape, f32),
+        in_specs=[pl.BlockSpec(memory_space=pltpu.HBM)] * len(operands),
         out_specs=pl.BlockSpec(memory_space=vmem),
         scratch_shapes=[
             vmem(height.shape, f32), vmem(height.shape, f32), vmem(height.shape, f32),
@@ -400,11 +485,13 @@
             vmem((2, 2, levels, nlon), f32), vmem((2, levels, nlon), f32), vmem(height.shape, f32),
             vmem((levels, nlon), f32), vmem((levels, nlon), f32), vmem((rows, 8, 2 * HALF), f32),
             vmem((tiles, 2 * most, 2 * HALF), bf16), vmem((tiles, most, 2 * HALF), f32),
-            vmem((8, HALF), f32), vmem((NX * NC, 8, HALF), f32), vmem((8, HALF), f32), vmem((7, 8, HALF), f32),
+            vmem((8, HALF), f32), vmem((NX * NC, 8, HALF), f32), vmem((8, HALF), f32), vmem((NY, 8, HALF), f32),
+            vmem((8, HALF), f32), vmem((8, HALF), f32),
             dma((11,)), dma((len(chunks), 2, 2)), dma((len(chunks), 2, 2)),
-            dma((NX * NC,)), dma((NX * NC,)), dma((7,)), dma((7,)),
+            dma, dma((NX * NC,)), dma((NY,)), dma((NY,)), dma((NX * NC,)), dma,
+            pltpu.SemaphoreType.REGULAR, pltpu.SemaphoreType.REGULAR((NY - 1,)),
         ],
-        compiler_params=pltpu.CompilerParams(collective_id=0, has_side_effects=True),
+        compiler_params=pltpu.CompilerParams(collective_id=0, has_side_effects=True, vmem_limit_bytes=16 * 2**20),
         name="advect_filter",
     )(*operands)
 

time: 42.6 us -> 35.2 us (0.83)
  the two profiles are of different devices: /device:TPU:515 before, /device:TPU:513 now
where the time goes in v2:
time: 35.2 us; the launch traced here: 35.1 us
  Pallas kernels  34.2 us (97%)
  local copies, waits for them, and re-layouts  0.88 us (2%)
    pallas_call x1, Pallas kernels, local(): pl.pallas_call(functools.partial(kernel, dims, nlon * cos_sum, chunks), o...  34.2 us
    unnamed x1, local copies, waits for them, and re-layouts  0.88 us

profile of v2, /device:TPU:513, one launch (start us, length us, event | category | flops | bytes accessed | tf_op | source)
XLA Modules:
  0.0 35.1 jit_solution(4006444704392265896)
XLA Ops:
  0.0 34.2 %advect_filter.1 = f32[4,32,1440]{2,1,0:T(8,128)S(1)} custom-call(f32[4,32,1440]{2,1,0:T(8,128)} %h_hbm.1, f32[4,32,1440]{2,1,0:T(8,128)} %z_hbm.1, f32[4,32,1440]{2,1,0:T(8,128)} %c_hbm.1, f32[32]{0:T(128)} %rates_hbm.1, f32[32]{0:T(128)} %thr_hbm.1, s32[512]{0:T(512)} %flags_hbm.1, s32[512]{0:T(512)} %cut_hbm.1, f32[1664]{0:T(1024)} %constant.8.clone.scal_hbm, ...), custom_call_target="tpu_custom_call" | custom-call | tf_op jit(solution)/shard_map/advect_filter/pallas_call | solution.py:475
  34.2 0.9 %copy.13 = f32[4,32,1440]{2,1,0:T(8,128)} copy(f32[4,32,1440]{2,1,0:T(8,128)S(1)} %advect_filter.1) | data formatting | bytes 1474560

commit v3 on v2

--- a/solution.py
+++ b/solution.py
@@ -103,13 +103,13 @@
 
 
 def kernel(
-    dims, area, chunks,
+    dims, area,
     h_hbm, z_hbm, c_hbm, rates_hbm, thr_hbm, flags_hbm, cut_hbm, scal_hbm, ksq_hbm, fwd_hbm, inv_hbm,
     out,
     h, z, c, rates, thr, flags, cut, scal, ksq, fwd, inv,
     halo_h, halo_c, base, s_lo, s_hi, factor, ymat, wmat, part, xbuf, ysum, ybuf,
     mean, mean_in,
-    in_sem, halo_send, halo_recv, x_send, x_recv, y_send, y_recv, mean_send, mean_recv, low_in, root_in,
+    in_sem, halo_send, halo_recv, x_send, x_recv, y_send, y_recv, mean_send, mean_recv, low_in, below_in, above_in,
 ):
     rows, levels, nlon, nlat = dims
     count = nlon // RADIX
@@ -117,19 +117,16 @@
     position = (x * NY + y) * NC + core
     total = NX * NY * NC
 
-    local = [
-        pltpu.make_async_copy(src, dst, in_sem.at[i])
-        for i, (src, dst) in enumerate(
-            [
-                (h_hbm, h), (c_hbm, c), (rates_hbm, rates), (thr_hbm, thr), (scal_hbm, scal), (z_hbm, z),
-                (flags_hbm, flags), (cut_hbm, cut), (ksq_hbm, ksq), (fwd_hbm, fwd), (inv_hbm, inv),
-            ]
-        )
-    ]
-    for copy in local:
+    pairs = [(h_hbm.at[r], h.at[r]) for r in range(rows)]
+    pairs += [(rates_hbm, rates), (thr_hbm, thr), (scal_hbm, scal), (c_hbm, c), (z_hbm, z)]
+    pairs += [(flags_hbm, flags), (cut_hbm, cut), (ksq_hbm, ksq), (fwd_hbm, fwd), (inv_hbm, inv)]
+    local = [pltpu.make_async_copy(src, dst, in_sem.at[i]) for i, (src, dst) in enumerate(pairs)]
+    h_in, small_in, c_in, z_in, rest_in = local[0:4], local[4:7], local[7], local[8], local[9:]
+    for copy in h_in + small_in + [c_in]:
         copy.start()
 
-    last = NX * NY * NC - 1
+    last = total - 1
+    first = position * rows
     is_root = jnp.logical_and(x == 0, core == 1)
 
     def along(step):
@@ -156,13 +153,13 @@
         for k in range(NX * NC):
             if k != 1:
                 signal(barrier, row(k))
-        for d in range(1, NY):
-
-            @pl.when(y >= d)
-            def _():
-                signal(barrier, column(-d))
-
-    pl.semaphore_wait(barrier, jnp.where(position < last, 1, 0) + jnp.where(is_root, NY - 1 - y, 1))
+
+        @pl.when(y > 0)
+        def _():
+            signal(barrier, column(-1))
+
+    greeted = jnp.where(is_root, jnp.where(y < NY - 1, 1, 0), 1) + jnp.where(position < last, 1, 0)
+    pl.semaphore_wait(barrier, greeted)
 
     @pl.when(position < last)
     def _():
@@ -170,35 +167,28 @@
 
     @pl.when(is_root)
     def _():
-        for d in range(1, NY):
-
-            @pl.when(y + d < NY)
-            def _():
-                signal(root_in.at[d - 1], column(d))
-
-    local[0].wait()
-    local[1].wait()
-
-    def halo_copies(i, side):
-        start, size = chunks[i]
-        lev = pl.ds(start, size)
+        @pl.when(y > 0)
+        def _():
+            pl.semaphore_wait(below_in, 1)
+
+        @pl.when(y < NY - 1)
+        def _():
+            signal(below_in, column(1))
+
+        @pl.when(y == NY - 1)
+        def _():
+            signal(above_in, column(-1))
+
+
+    def halo_copy(side, field):
         step, h_row, c_row = ((1, rows - 2, rows - 1), (-1, 0, 0))[side]
-        sems = [(halo_send.at[i, side, k], halo_recv.at[i, side, k]) for k in range(2)]
-        pairs = ((h.at[pl.ds(h_row, 2), lev], halo_h.at[side, :, lev]), (c.at[c_row, lev], halo_c.at[side, lev]))
-        return [
-            pltpu.make_async_remote_copy(
-                src, dst, send, recv, device_id=along(step), device_id_type=MESH
-            )
-            for (src, dst), (send, recv) in zip(pairs, sems)
-        ]
-
-    @pl.when(position < last)
-    def _():
-        for i in range(len(chunks)):
-            for copy in halo_copies(i, 0):
-                copy.start()
-
-    ymat[...] = jnp.zeros_like(ymat)
+        src = (h.at[pl.ds(h_row, 2)], c.at[c_row])[field]
+        dst = (halo_h.at[side], halo_c.at[side])[field]
+        return pltpu.make_async_remote_copy(
+            src, dst, halo_send.at[side, field], halo_recv.at[side, field], device_id=along(step), device_id_type=MESH
+        )
+
+    base[:, :, nlon:] = jnp.zeros((rows, levels, base.shape[2] - nlon), jnp.float32)
 
     @pl.when(position == 0)
     def _():
@@ -210,9 +200,12 @@
         halo_h[1] = jnp.zeros_like(halo_h[1])
         halo_c[1] = jnp.zeros_like(halo_c[1])
 
-    for i in (2, 3, 4):
-        local[i].wait()
-    first = position * rows
+    for copy in small_in + h_in:
+        copy.wait()
+
+    @pl.when(core == 0)
+    def _():
+        halo_copy(0, 0).start()
 
     lane = lax.broadcasted_iota(jnp.int32, (8, HALF), 1)
     tile = jnp.zeros((8, HALF), jnp.float32)
@@ -232,7 +225,7 @@
             height = h[r, lev, :]
             s = height - threshold
             source = -rate * (jnp.maximum(s, 0.0) + jnp.log(1.0 + jnp.exp(-jnp.abs(s))))
-            base[r, lev, :] = height + source
+            base[r, lev, 0:nlon] = height + source
             sums = sums + scal[first + r] * jnp.sum(source, axis=1, keepdims=True)
         tile = jnp.where(lane == g, sums, tile)
     part[...] = tile
@@ -246,14 +239,19 @@
     def _():
         part_copy(x * NC + core).start()
 
-    @pl.when(position > 0)
-    def _():
-        pl.semaphore_wait(low_in, 1)
-        for i in range(len(chunks)):
-            for copy in halo_copies(i, 1):
-                copy.start()
-
-    local[5].wait()
+    for copy in [z_in] + rest_in:
+        copy.start()
+    c_in.wait()
+
+    @pl.when(jnp.logical_and(core != 0, position < last))
+    def _():
+        halo_copy(0, 0).start()
+
+    @pl.when(position < last)
+    def _():
+        halo_copy(0, 1).start()
+
+    z_in.wait()
 
     def inv_cos(r):
         return scal[nlat + first + r]
@@ -284,13 +282,19 @@
             zr = z[r, lev, :]
             speed = zr + east(zr)
             flux = speed * (8.0 * pair - (west(pair) + east(pair))) * (1.0 / 24.0)
-            base[r, lev, :] = base[r, lev, :] - (flux - west(flux)) - terms[r] * inv_cos(r)
+            base[r, lev, 0:nlon] = base[r, lev, 0:nlon] - (flux - west(flux)) - terms[r] * inv_cos(r)
         return carry
 
     lax.fori_loop(0, levels // 8, local_terms, 0)
 
-    for i in (6, 7, 8):
-        local[i].wait()
+    @pl.when(position > 0)
+    def _():
+        pl.semaphore_wait(low_in, 1)
+        halo_copy(1, 0).start()
+        halo_copy(1, 1).start()
+
+    for copy in rest_in[0:3]:
+        copy.wait()
     for r in range(rows):
         cutoff = cut[first + r].astype(jnp.float32)
         flag = flags[first + r].astype(jnp.float32)
@@ -309,82 +313,93 @@
             mean, mean_in, mean_send.at[k], mean_recv, device_id=row(k), device_id_type=MESH
         )
 
-    @pl.when(is_root)
-    def _():
+    def gather_row():
+        for k in range(NX * NC):
+            if k != 1:
+                landed(xbuf.at[k], x_recv.at[k])
         acc = part[...]
         for k in range(NX * NC):
             if k != 1:
-                landed(xbuf.at[k], x_recv.at[k])
                 acc = acc + xbuf[k]
         ysum[...] = acc
         for d in range(1, NY):
-
-            @pl.when(y + d < NY)
-            def _():
-                sum_copy(d).start()
-
-        for d in range(1, NY):
-
-            @pl.when(y >= d)
-            def _():
-                pl.semaphore_wait(root_in.at[d - 1], 1)
-                sum_copy(-d).start()
-
-        mean[...] = acc
+            for step, used in ((d, y + d < NY), (-d, y >= d)):
+
+                @pl.when(used)
+                def _():
+                    sum_copy(step).start()
+
+    def spread_mean():
         for k in range(NY):
 
             @pl.when(y != k)
             def _():
                 landed(ybuf.at[k], y_recv.at[k])
-                mean[...] = mean[...] + ybuf[k]
-
-        mean[...] = mean[...] * (1.0 / area)
+
+        acc = ysum[...]
+        for k in range(NY):
+            acc = acc + jnp.where(y != k, ybuf[k], 0.0)
+        mean[...] = acc * (1.0 / area)
         for k in range(NX * NC):
             if k != 1:
                 mean_copy(k).start()
-        mean_in[...] = mean[...]
-
-    local[9].wait()
-    local[10].wait()
-    for i, (start, size) in enumerate(chunks):
-        @pl.when(position > 0)
-        def _():
-            for copy in halo_copies(i, 0):
-                copy.wait_recv()
-
-        @pl.when(position < last)
-        def _():
-            for copy in halo_copies(i, 1):
-                copy.wait_recv()
-
-        def edges(g, carry):
-            lev = pl.ds(pl.multiple_of(start + 8 * g, 8), 8)
-            h0, h1, h2, h3 = (h[r, lev, :] for r in range(rows))
-            below, below2 = halo_h[0, 1, lev, :], halo_h[0, 0, lev, :]
-            above, above2 = halo_h[1, 0, lev, :], halo_h[1, 1, lev, :]
-            t1 = s_lo[lev, :] * below
-            t3 = s_hi[lev, :] * above
-            f0 = face(0) * (halo_c[0, lev, :] + c[0, lev, :]) * (7.0 * (below + h0) - (below2 + h1))
-            f4 = face(4) * (halo_c[1, lev, :] + c[3, lev, :]) * (7.0 * (above + h3) - (above2 + h2))
-            base[0, lev, :] = base[0, lev, :] + (t1 + f0) * inv_cos(0)
-            base[1, lev, :] = base[1, lev, :] - t1 * inv_cos(1)
-            base[2, lev, :] = base[2, lev, :] + t3 * inv_cos(2)
-            base[3, lev, :] = base[3, lev, :] - (t3 + f4) * inv_cos(3)
-            return carry
-
-        lax.fori_loop(0, size // 8, edges, 0)
-
-        blocks = size // 16
-        units = rows * size
-
+        mean_in[...] = acc * (1.0 / area)
+
+    @pl.when(is_root)
+    def _():
+        @pl.when(y < NY - 1)
+        def _():
+            pl.semaphore_wait(above_in, 1)
+
+            @pl.when(y > 0)
+            def _():
+                signal(above_in, column(-1))
+
+        @pl.when(y > 0)
+        def _():
+            gather_row()
+
+    for copy in rest_in[3:]:
+        copy.wait()
+    lanes = lax.broadcasted_iota(jnp.int32, (16, HALF), 1)
+    units = 2 * levels
+    blocks = levels // 16
+
+    def edges_above(g, carry):
+        lev = pl.ds(pl.multiple_of(8 * g, 8), 8)
+        above, above2 = halo_h[1, 0, lev, :], halo_h[1, 1, lev, :]
+        t3 = s_hi[lev, :] * above
+        f4 = face(4) * (halo_c[1, lev, :] + c[3, lev, :]) * (7.0 * (above + h[3, lev, :]) - (above2 + h[2, lev, :]))
+        base[2, lev, 0:nlon] = base[2, lev, 0:nlon] + t3 * inv_cos(2)
+        base[3, lev, 0:nlon] = base[3, lev, 0:nlon] - (t3 + f4) * inv_cos(3)
+        return carry
+
+    def edges_below(g, carry):
+        lev = pl.ds(pl.multiple_of(8 * g, 8), 8)
+        below, below2 = halo_h[0, 1, lev, :], halo_h[0, 0, lev, :]
+        t1 = s_lo[lev, :] * below
+        f0 = face(0) * (halo_c[0, lev, :] + c[0, lev, :]) * (7.0 * (below + h[0, lev, :]) - (below2 + h[1, lev, :]))
+        base[0, lev, 0:nlon] = base[0, lev, 0:nlon] + (t1 + f0) * inv_cos(0)
+        base[1, lev, 0:nlon] = base[1, lev, 0:nlon] - t1 * inv_cos(1)
+        return carry
+
+    def product(hilo, table):
+        first_part = jnp.dot(hilo, table[0], preferred_element_type=jnp.float32)
+        second = jnp.dot(hilo[0:units], table[1], preferred_element_type=jnp.float32)
+        return first_part[0:units] + first_part[units : 2 * units] + second
+
+    def filter_rows(row0):
         def block_of(b):
-            r = b // blocks
-            lev = pl.ds(pl.multiple_of(start + 16 * lax.rem(b, blocks), 16), 16)
-            return r, lev, pl.ds(pl.multiple_of(16 * b, 16), 16), pl.ds(pl.multiple_of(units + 16 * b, 16), 16)
+            lev = pl.ds(pl.multiple_of(16 * lax.rem(b, blocks), 16), 16)
+            at_hi, at_lo = pl.multiple_of(16 * b, 16), pl.multiple_of(units + 16 * b, 16)
+            return row0 + b // blocks, lev, pl.ds(at_hi, 16), pl.ds(at_lo, 16)
 
         def forward(b, carry):
             r, lev, at_hi, at_lo = block_of(b)
-            u = [base[r, lev, count * j : count * (j + 1)] for j in range(RADIX)]
+            v = [base[r, lev, HALF * j : HALF * (j + 1)] for j in range(RADIX)]
+            u = [v[0]] + [
+                pltpu.roll(jnp.where(lanes >= HALF - 8 * j, v[j - 1], v[j]), 8 * j, axis=1) for j in range(1, RADIX)
+            ]
             e = [u[0]] + [u[j] + u[RADIX - j] for j in range(1, 6)] + [u[6]]
             o = [u[j] - u[RADIX - j] for j in range(1, 6)]
             even, odd = twelve(e, o)
@@ -392,36 +407,59 @@
             for m, pair in enumerate(halves):
                 for k, value in enumerate(pair):
                     hi, lo = split(value)
-                    ymat[m, at_hi, HALF * k : HALF * k + count] = hi
-                    ymat[m, at_lo, HALF * k : HALF * k + count] = lo
+                    ymat[m, at_hi, HALF * k : HALF * (k + 1)] = hi
+                    ymat[m, at_lo, HALF * k : HALF * (k + 1)] = lo
             return carry
-
-        lax.fori_loop(0, rows * blocks, forward, 0)
-
-        def product(hilo, table):
-            first_part = jnp.dot(hilo, table[0], preferred_element_type=jnp.float32)
-            second = jnp.dot(hilo[0:units], table[1], preferred_element_type=jnp.float32)
-            return first_part[0:units] + first_part[units : 2 * units] + second
-
-        for m in range(RADIX // 2):
-            waves = product(ymat[m, 0 : 2 * units, :], (fwd[0, m], fwd[1, m]))
-            scaled = jnp.concatenate(
-                [waves[r * size : (r + 1) * size] * factor[r, m : m + 1, :] for r in range(rows)], axis=0
-            )
-            wmat[m, 0:units, :] = product(jnp.concatenate(split(scaled), axis=0), (inv[0, m], inv[1, m]))
 
         def backward(b, carry):
             r, lev, at, _ = block_of(b)
-            w = [[wmat[m, at, HALF * k : HALF * k + count] for k in range(2)] for m in range(RADIX // 2)]
+            w = [[wmat[m, at, HALF * k : HALF * (k + 1)] for k in range(2)] for m in range(RADIX // 2)]
             even, odd = twelve([w[0][0]] + [w[m][0] for m in range(1, 6)] + [w[0][1]], [w[m][1] for m in range(1, 6)])
             removed = [even[0]] + [even[j] + odd[j - 1] for j in range(1, 6)] + [even[6]]
             removed += [even[RADIX - j] - odd[RADIX - j - 1] for j in range(7, RADIX)]
+            back = [removed[0]] + [pltpu.roll(removed[j], HALF - 8 * j, axis=1) for j in range(1, RADIX)]
             for j in range(RADIX):
-                cols = slice(count * j, count * (j + 1))
-                out[r, lev, cols] = base[r, lev, cols] - removed[j]
+                if j < RADIX - 1:
+                    piece = jnp.where(lanes < count - 8 * j, back[j], back[j + 1])
+                    out[r, lev, HALF * j : HALF * (j + 1)] = base[r, lev, HALF * j : HALF * (j + 1)] - piece
+                else:
+                    left = base[r, lev, HALF * j : HALF * (j + 1)] - back[j]
+                    out[r, lev, HALF * j : nlon] = left[:, 0 : nlon - HALF * j]
             return carry
 
-        lax.fori_loop(0, rows * blocks, backward, 0)
+        lax.fori_loop(0, 2 * blocks, forward, 0)
+        for m in range(RADIX // 2):
+            waves = product(ymat[m], (fwd[0, m], fwd[1, m]))
+            scaled = jnp.concatenate(
+                [waves[r * levels : (r + 1) * levels] * factor[row0 + r, m : m + 1, :] for r in range(2)], axis=0
+            )
+            wmat[m] = product(jnp.concatenate(split(scaled), axis=0), (inv[0, m], inv[1, m]))
+        lax.fori_loop(0, 2 * blocks, backward, 0)
+
+    @pl.when(position < last)
+    def _():
+        halo_copy(1, 0).wait_recv()
+        halo_copy(1, 1).wait_recv()
+
+    lax.fori_loop(0, levels // 8, edges_above, 0)
+    filter_rows(2)
+
+    @pl.when(jnp.logical_and(is_root, y == 0))
+    def _():
+        gather_row()
+        spread_mean()
+
+    @pl.when(position > 0)
+    def _():
+        halo_copy(0, 0).wait_recv()
+        halo_copy(0, 1).wait_recv()
+
+    lax.fori_loop(0, levels // 8, edges_below, 0)
+    filter_rows(0)
+
+    @pl.when(jnp.logical_and(is_root, y > 0))
+    def _():
+        spread_mean()
 
     @pl.when(jnp.logical_not(is_root))
     def _():
@@ -437,9 +475,8 @@
 
         @pl.when(sender)
         def _():
-            for i in range(len(chunks)):
-                for copy in halo_copies(i, side):
-                    copy.wait_send()
+            halo_copy(side, 0).wait_send()
+            halo_copy(side, 1).wait_send()
 
     @pl.when(is_root)
     def _():
@@ -464,8 +501,6 @@
     nlat = rows * NX * NY * NC
     fwd, inv, ksq = filter_tables(nlon)
     scalars, cos_sum = row_scalars(nlat)
-    chunks = ((0, levels // 2), (levels // 2, levels // 2))
-    most = rows * max(size for _, size in chunks)
     tiles = RADIX // 2
     dims = (rows, levels, nlon, nlat)
     f32, bf16 = jnp.float32, jnp.bfloat16
@@ -473,7 +508,7 @@
     operands = (height, zonal, merid, rates, thresholds, flags, cutoffs, scalars, ksq, fwd, inv)
     operands = [pltpu.with_memory_space_constraint(jnp.asarray(a), pltpu.HBM) for a in operands]
     return pl.pallas_call(
-        functools.partial(kernel, dims, nlon * cos_sum, chunks),
+        functools.partial(kernel, dims, nlon * cos_sum),
         out_shape=vmem(height.shape, f32),
         in_specs=[pl.BlockSpec(memory_space=pltpu.HBM)] * len(operands),
         out_specs=pl.BlockSpec(memory_space=vmem),
@@ -482,14 +517,14 @@
             smem(rates.shape, f32), smem(thresholds.shape, f32), smem(flags.shape, jnp.int32),
             smem(cutoffs.shape, jnp.int32), smem(scalars.shape, f32),
             vmem(ksq.shape, f32), vmem(fwd.shape, bf16), vmem(inv.shape, bf16),
-            vmem((2, 2, levels, nlon), f32), vmem((2, levels, nlon), f32), vmem(height.shape, f32),
+            vmem((2, 2, levels, nlon), f32), vmem((2, levels, nlon), f32), vmem((rows, levels, RADIX * HALF), f32),
             vmem((levels, nlon), f32), vmem((levels, nlon), f32), vmem((rows, 8, 2 * HALF), f32),
-            vmem((tiles, 2 * most, 2 * HALF), bf16), vmem((tiles, most, 2 * HALF), f32),
+            vmem((tiles, 4 * levels, 2 * HALF), bf16), vmem((tiles, 2 * levels, 2 * HALF), f32),
             vmem((8, HALF), f32), vmem((NX * NC, 8, HALF), f32), vmem((8, HALF), f32), vmem((NY, 8, HALF), f32),
             vmem((8, HALF), f32), vmem((8, HALF), f32),
-            dma((11,)), dma((len(chunks), 2, 2)), dma((len(chunks), 2, 2)),
+            dma((14,)), dma((2, 2)), dma((2, 2)),
             dma, dma((NX * NC,)), dma((NY,)), dma((NY,)), dma((NX * NC,)), dma,
-            pltpu.SemaphoreType.REGULAR, pltpu.SemaphoreType.REGULAR((NY - 1,)),
+            *[pltpu.SemaphoreType.REGULAR] * 3,
         ],
         compiler_params=pltpu.CompilerParams(collective_id=0, has_side_effects=True, vmem_limit_bytes=16 * 2**20),
         name="advect_filter",

time: 35.2 us -> 28.4 us (0.81)
  Pallas kernels: 34.2 us -> 27.4 us
    pallas_call x1, Pallas kernels: 34.2 us -> 27.4 us  [local(): pl.pallas_call(functools.partial(kernel, dims, nlon * cos_sum), out_shape...]
where the time goes in v3:
time: 28.4 us; the launch traced here: 28.3 us
  Pallas kernels  27.4 us (96%)
  local copies, waits for them, and re-layouts  0.88 us (3%)
    pallas_call x1, Pallas kernels, local(): pl.pallas_call(functools.partial(kernel, dims, nlon * cos_sum), out_shape...  27.4 us
    unnamed x1, local copies, waits for them, and re-layouts  0.88 us

profile of v3, /device:TPU:513, one launch (start us, length us, event | category | flops | bytes accessed | tf_op | source)
XLA Modules:
  0.0 28.3 jit_solution(10582332020019936923)
XLA Ops:
  0.0 27.4 %advect_filter.1 = f32[4,32,1440]{2,1,0:T(8,128)S(1)} custom-call(f32[4,32,1440]{2,1,0:T(8,128)} %h_hbm.1, f32[4,32,1440]{2,1,0:T(8,128)} %z_hbm.1, f32[4,32,1440]{2,1,0:T(8,128)} %c_hbm.1, f32[32]{0:T(128)} %rates_hbm.1, f32[32]{0:T(128)} %thr_hbm.1, s32[512]{0:T(512)} %flags_hbm.1, s32[512]{0:T(512)} %cut_hbm.1, f32[1664]{0:T(1024)} %constant.8.clone.scal_hbm, ...), custom_call_target="tpu_custom_call" | custom-call | tf_op jit(solution)/shard_map/advect_filter/pallas_call | solution.py:510
  27.4 0.9 %copy.13 = f32[4,32,1440]{2,1,0:T(8,128)} copy(f32[4,32,1440]{2,1,0:T(8,128)S(1)} %advect_filter.1) | data formatting | bytes 1474560

commit v4 on v3

--- a/solution.py
+++ b/solution.py
@@ -108,8 +108,8 @@
     out,
     h, z, c, rates, thr, flags, cut, scal, ksq, fwd, inv,
     halo_h, halo_c, base, s_lo, s_hi, factor, ymat, wmat, part, xbuf, ysum, ybuf,
-    mean, mean_in,
-    in_sem, halo_send, halo_recv, x_send, x_recv, y_send, y_recv, mean_send, mean_recv, low_in, below_in, above_in,
+    mean_in, level_rates, level_thresholds,
+    in_sem, halo_send, halo_recv, x_send, x_recv, y_send, y_recv, mean_send, mean_recv, low_in,
 ):
     rows, levels, nlon, nlat = dims
     count = nlon // RADIX
@@ -128,6 +128,8 @@
     last = total - 1
     first = position * rows
     is_root = jnp.logical_and(x == 0, core == 1)
+    is_first = position == 1
+    is_later_root = jnp.logical_and(is_root, y > 0)
 
     def along(step):
         p = lax.rem(position + total + step, total)
@@ -136,8 +138,8 @@
     def row(k):
         return {"lat_0": jnp.int32(k // NC), "lat_1": y, "lat_2": jnp.int32(k % NC)}
 
-    def column(d):
-        return {"lat_0": jnp.int32(0), "lat_1": y + d, "lat_2": jnp.int32(1)}
+    def root(k):
+        return {"lat_0": jnp.int32(0), "lat_1": jnp.int32(k), "lat_2": jnp.int32(1)}
 
     def signal(sem, device):
         pl.semaphore_signal(sem, inc=1, device_id=device, device_id_type=MESH)
@@ -154,31 +156,17 @@
             if k != 1:
                 signal(barrier, row(k))
 
-        @pl.when(y > 0)
-        def _():
-            signal(barrier, column(-1))
-
-    greeted = jnp.where(is_root, jnp.where(y < NY - 1, 1, 0), 1) + jnp.where(position < last, 1, 0)
+    @pl.when(is_first)
+    def _():
+        for k in range(1, NY):
+            signal(barrier, root(k))
+
+    greeted = jnp.where(is_first, 0, 1) + jnp.where(position < last, 1, 0)
     pl.semaphore_wait(barrier, greeted)
 
     @pl.when(position < last)
     def _():
         signal(low_in, along(1))
-
-    @pl.when(is_root)
-    def _():
-        @pl.when(y > 0)
-        def _():
-            pl.semaphore_wait(below_in, 1)
-
-        @pl.when(y < NY - 1)
-        def _():
-            signal(below_in, column(1))
-
-        @pl.when(y == NY - 1)
-        def _():
-            signal(above_in, column(-1))
-
 
     def halo_copy(side, field):
         step, h_row, c_row = ((1, rows - 2, rows - 1), (-1, 0, 0))[side]
@@ -217,17 +205,23 @@
             value = jnp.where(sub == k, ref[start + k], value)
         return value
 
+    full = nlon // HALF
     for g in range(levels // 8):
         lev = pl.ds(8 * g, 8)
         rate, threshold = levels_of(rates, 8 * g), levels_of(thr, 8 * g)
-        sums = jnp.zeros((8, 1), jnp.float32)
+        wide, rest = 0.0, 0.0
         for r in range(rows):
-            height = h[r, lev, :]
-            s = height - threshold
-            source = -rate * (jnp.maximum(s, 0.0) + jnp.log(1.0 + jnp.exp(-jnp.abs(s))))
-            base[r, lev, 0:nlon] = height + source
-            sums = sums + scal[first + r] * jnp.sum(source, axis=1, keepdims=True)
-        tile = jnp.where(lane == g, sums, tile)
+            positive, factors = 0.0, 1.0
+            for j in range(full):
+                s = h[r, lev, HALF * j : HALF * (j + 1)] - threshold
+                positive = positive + jnp.maximum(s, 0.0)
+                factors = factors * (1.0 + jnp.exp(-jnp.abs(s)))
+            s = h[r, lev, HALF * full : nlon] - threshold
+            wide = wide + scal[first + r] * (positive + jnp.log(factors))
+            rest = rest + scal[first + r] * (jnp.maximum(s, 0.0) + jnp.log(1.0 + jnp.exp(-jnp.abs(s))))
+        sums = jnp.sum(wide, axis=1, keepdims=True) + jnp.sum(rest, axis=1, keepdims=True)
+        tile = jnp.where(lane == g, -rate * sums, tile)
+        level_rates[g], level_thresholds[g] = jnp.broadcast_to(rate, (8, HALF)), jnp.broadcast_to(threshold, (8, HALF))
     part[...] = tile
 
     def part_copy(slot):
@@ -268,6 +262,7 @@
     def local_terms(g, carry):
         lev = pl.ds(pl.multiple_of(8 * g, 8), 8)
         hr = [h[r, lev, :] for r in range(rows)]
+        rate, threshold = level_rates[g][:, 0:1], level_thresholds[g][:, 0:1]
         cr = [c[r, lev, :] for r in range(rows)]
         low = face(1) * (cr[0] + cr[1])
         high = face(3) * (cr[2] + cr[3])
@@ -282,7 +277,9 @@
             zr = z[r, lev, :]
             speed = zr + east(zr)
             flux = speed * (8.0 * pair - (west(pair) + east(pair))) * (1.0 / 24.0)
-            base[r, lev, 0:nlon] = base[r, lev, 0:nlon] - (flux - west(flux)) - terms[r] * inv_cos(r)
+            s = hr[r] - threshold
+            source = rate * (jnp.maximum(s, 0.0) + jnp.log(1.0 + jnp.exp(-jnp.abs(s))))
+            base[r, lev, 0:nlon] = (hr[r] - source) - (flux - west(flux)) - terms[r] * inv_cos(r)
         return carry
 
     lax.fori_loop(0, levels // 8, local_terms, 0)
@@ -303,61 +300,34 @@
     def landed(ref, sem):
         pltpu.make_async_copy(ref, ref, sem).wait()
 
-    def sum_copy(d):
+    def sum_copy():
         return pltpu.make_async_remote_copy(
-            ysum, ybuf.at[y], y_send.at[y + d], y_recv.at[y], device_id=column(d), device_id_type=MESH
+            ysum, ybuf.at[y], y_send, y_recv.at[y], device_id=root(0), device_id_type=MESH
         )
 
-    def mean_copy(k):
+    def mean_copy(slot, device):
         return pltpu.make_async_remote_copy(
-            mean, mean_in, mean_send.at[k], mean_recv, device_id=row(k), device_id_type=MESH
+            mean_in, mean_in, mean_send.at[slot], mean_recv, device_id=device, device_id_type=MESH
         )
 
+    members = [0] + [k for d in (4, 3, 5, 2, 6, 1, 7) for k in (NC * d, NC * d + 1)]
+
     def gather_row():
-        for k in range(NX * NC):
-            if k != 1:
-                landed(xbuf.at[k], x_recv.at[k])
+        for k in members:
+            landed(xbuf.at[k], x_recv.at[k])
         acc = part[...]
-        for k in range(NX * NC):
-            if k != 1:
-                acc = acc + xbuf[k]
-        ysum[...] = acc
-        for d in range(1, NY):
-            for step, used in ((d, y + d < NY), (-d, y >= d)):
-
-                @pl.when(used)
-                def _():
-                    sum_copy(step).start()
-
-    def spread_mean():
-        for k in range(NY):
-
-            @pl.when(y != k)
-            def _():
-                landed(ybuf.at[k], y_recv.at[k])
-
-        acc = ysum[...]
-        for k in range(NY):
-            acc = acc + jnp.where(y != k, ybuf[k], 0.0)
-        mean[...] = acc * (1.0 / area)
-        for k in range(NX * NC):
-            if k != 1:
-                mean_copy(k).start()
-        mean_in[...] = acc * (1.0 / area)
-
-    @pl.when(is_root)
-    def _():
-        @pl.when(y < NY - 1)
-        def _():
-            pl.semaphore_wait(above_in, 1)
-
-            @pl.when(y > 0)
-            def _():
-                signal(above_in, column(-1))
-
-        @pl.when(y > 0)
-        def _():
-            gather_row()
+        for k in members:
+            acc = acc + xbuf[k]
+        return acc
+
+    def spread_row():
+        for k in members[1:] + members[:1]:
+            mean_copy(k, row(k)).start()
+
+    @pl.when(is_later_root)
+    def _():
+        ysum[...] = gather_row()
+        sum_copy().start()
 
     for copy in rest_in[3:]:
         copy.wait()
@@ -390,11 +360,9 @@
 
     def filter_rows(row0):
         def block_of(b):
-            lev = pl.ds(pl.multiple_of(16 * lax.rem(b, blocks), 16), 16)
-            at_hi, at_lo = pl.multiple_of(16 * b, 16), pl.multiple_of(units + 16 * b, 16)
-            return row0 + b // blocks, lev, pl.ds(at_hi, 16), pl.ds(at_lo, 16)
-
-        def forward(b, carry):
+            return row0 + b // blocks, pl.ds(16 * (b % blocks), 16), pl.ds(16 * b, 16), pl.ds(units + 16 * b, 16)
+
+        def forward(b):
             r, lev, at_hi, at_lo = block_of(b)
             v = [base[r, lev, HALF * j : HALF * (j + 1)] for j in range(RADIX)]
             u = [v[0]] + [
@@ -409,9 +377,8 @@
                     hi, lo = split(value)
                     ymat[m, at_hi, HALF * k : HALF * (k + 1)] = hi
                     ymat[m, at_lo, HALF * k : HALF * (k + 1)] = lo
-            return carry
-
-        def backward(b, carry):
+
+        def backward(b):
             r, lev, at, _ = block_of(b)
             w = [[wmat[m, at, HALF * k : HALF * (k + 1)] for k in range(2)] for m in range(RADIX // 2)]
             even, odd = twelve([w[0][0]] + [w[m][0] for m in range(1, 6)] + [w[0][1]], [w[m][1] for m in range(1, 6)])
@@ -425,16 +392,17 @@
                 else:
                     left = base[r, lev, HALF * j : HALF * (j + 1)] - back[j]
                     out[r, lev, HALF * j : nlon] = left[:, 0 : nlon - HALF * j]
-            return carry
-
-        lax.fori_loop(0, 2 * blocks, forward, 0)
+
+        for b in range(2 * blocks):
+            forward(b)
         for m in range(RADIX // 2):
             waves = product(ymat[m], (fwd[0, m], fwd[1, m]))
             scaled = jnp.concatenate(
                 [waves[r * levels : (r + 1) * levels] * factor[row0 + r, m : m + 1, :] for r in range(2)], axis=0
             )
             wmat[m] = product(jnp.concatenate(split(scaled), axis=0), (inv[0, m], inv[1, m]))
-        lax.fori_loop(0, 2 * blocks, backward, 0)
+        for b in range(2 * blocks):
+            backward(b)
 
     @pl.when(position < last)
     def _():
@@ -444,10 +412,17 @@
     lax.fori_loop(0, levels // 8, edges_above, 0)
     filter_rows(2)
 
-    @pl.when(jnp.logical_and(is_root, y == 0))
-    def _():
-        gather_row()
-        spread_mean()
+    @pl.when(is_first)
+    def _():
+        for k in range(1, NY):
+            landed(ybuf.at[k], y_recv.at[k])
+        acc = ybuf[1]
+        for k in range(2, NY):
+            acc = acc + ybuf[k]
+        mean_in[...] = (gather_row() + acc) * (1.0 / area)
+        spread_row()
+        for k in range(1, NY):
+            mean_copy(NX * NC + k, root(k)).start()
 
     @pl.when(position > 0)
     def _():
@@ -457,13 +432,13 @@
     lax.fori_loop(0, levels // 8, edges_below, 0)
     filter_rows(0)
 
-    @pl.when(jnp.logical_and(is_root, y > 0))
-    def _():
-        spread_mean()
-
-    @pl.when(jnp.logical_not(is_root))
-    def _():
-        mean_copy(0).wait_recv()
+    @pl.when(jnp.logical_not(is_first))
+    def _():
+        mean_copy(0, row(0)).wait_recv()
+
+    @pl.when(is_later_root)
+    def _():
+        spread_row()
 
     for g in range(levels // 8):
         lev = pl.ds(8 * g, 8)
@@ -478,18 +453,19 @@
             halo_copy(side, 0).wait_send()
             halo_copy(side, 1).wait_send()
 
+    @pl.when(is_later_root)
+    def _():
+        sum_copy().wait_send()
+
     @pl.when(is_root)
     def _():
-        for d in range(1, NY):
-            for step, used in ((d, y + d < NY), (-d, y >= d)):
-
-                @pl.when(used)
-                def _():
-                    sum_copy(step).wait_send()
-
-        for k in range(NX * NC):
-            if k != 1:
-                mean_copy(k).wait_send()
+        for k in members:
+            mean_copy(k, row(k)).wait_send()
+
+    @pl.when(is_first)
+    def _():
+        for k in range(1, NY):
+            mean_copy(NX * NC + k, root(k)).wait_send()
 
     @pl.when(jnp.logical_not(is_root))
     def _():
@@ -521,10 +497,9 @@
             vmem((levels, nlon), f32), vmem((levels, nlon), f32), vmem((rows, 8, 2 * HALF), f32),
             vmem((tiles, 4 * levels, 2 * HALF), bf16), vmem((tiles, 2 * levels, 2 * HALF), f32),
             vmem((8, HALF), f32), vmem((NX * NC, 8, HALF), f32), vmem((8, HALF), f32), vmem((NY, 8, HALF), f32),
-            vmem((8, HALF), f32), vmem((8, HALF), f32),
+            vmem((8, HALF), f32), vmem((levels // 8, 8, HALF), f32), vmem((levels // 8, 8, HALF), f32),
             dma((14,)), dma((2, 2)), dma((2, 2)),
-            dma, dma((NX * NC,)), dma((NY,)), dma((NY,)), dma((NX * NC,)), dma,
-            *[pltpu.SemaphoreType.REGULAR] * 3,
+            dma, dma((NX * NC,)), dma, dma((NY,)), dma((NX * NC + NY,)), dma, pltpu.SemaphoreType.REGULAR,
         ],
         compiler_params=pltpu.CompilerParams(collective_id=0, has_side_effects=True, vmem_limit_bytes=16 * 2**20),
         name="advect_filter",

time: 28.4 us -> 26.3 us (0.926)
  Pallas kernels: 27.4 us -> 25.3 us
    pallas_call x1, Pallas kernels: 27.4 us -> 25.3 us  [local(): pl.pallas_call(functools.partial(kernel, dims, nlon * cos_sum), out_shape...]
where the time goes in v4:
time: 26.3 us; the launch traced here: 26.2 us
  Pallas kernels  25.3 us (96%)
  local copies, waits for them, and re-layouts  0.88 us (3%)
    pallas_call x1, Pallas kernels, local(): pl.pallas_call(functools.partial(kernel, dims, nlon * cos_sum), out_shape...  25.3 us
    unnamed x1, local copies, waits for them, and re-layouts  0.88 us

profile of v4, /device:TPU:513, one launch (start us, length us, event | category | flops | bytes accessed | tf_op | source)
XLA Modules:
  0.0 26.2 jit_solution(14231768117148082349)
XLA Ops:
  0.0 25.3 %advect_filter.1 = f32[4,32,1440]{2,1,0:T(8,128)S(1)} custom-call(f32[4,32,1440]{2,1,0:T(8,128)} %h_hbm.1, f32[4,32,1440]{2,1,0:T(8,128)} %z_hbm.1, f32[4,32,1440]{2,1,0:T(8,128)} %c_hbm.1, f32[32]{0:T(128)} %rates_hbm.1, f32[32]{0:T(128)} %thr_hbm.1, s32[512]{0:T(512)} %flags_hbm.1, s32[512]{0:T(512)} %cut_hbm.1, f32[1664]{0:T(1024)} %constant.8.clone.scal_hbm, ...), custom_call_target="tpu_custom_call" | custom-call | tf_op jit(solution)/shard_map/advect_filter/pallas_call | solution.py:486
  25.3 0.9 %copy.13 = f32[4,32,1440]{2,1,0:T(8,128)} copy(f32[4,32,1440]{2,1,0:T(8,128)S(1)} %advect_filter.1) | data formatting | bytes 1474560

commit v5 on v4

--- a/solution.py
+++ b/solution.py
@@ -107,9 +107,8 @@
     h_hbm, z_hbm, c_hbm, rates_hbm, thr_hbm, flags_hbm, cut_hbm, scal_hbm, ksq_hbm, fwd_hbm, inv_hbm,
     out,
     h, z, c, rates, thr, flags, cut, scal, ksq, fwd, inv,
-    halo_h, halo_c, base, s_lo, s_hi, factor, ymat, wmat, part, xbuf, ysum, ybuf,
-    mean_in, level_rates, level_thresholds,
-    in_sem, halo_send, halo_recv, x_send, x_recv, y_send, y_recv, mean_send, mean_recv, low_in,
+    halo, base, s_lo, s_hi, factor, ymat, wmat, part, box, mean_in, level_rates, level_thresholds,
+    in_sem, halo_send, halo_recv, up_send, x_recv, y_recv, mean_send, mean_recv, low_in,
 ):
     rows, levels, nlon, nlat = dims
     count = nlon // RADIX
@@ -117,12 +116,18 @@
     position = (x * NY + y) * NC + core
     total = NX * NY * NC
 
-    pairs = [(h_hbm.at[r], h.at[r]) for r in range(rows)]
-    pairs += [(rates_hbm, rates), (thr_hbm, thr), (scal_hbm, scal), (c_hbm, c), (z_hbm, z)]
-    pairs += [(flags_hbm, flags), (cut_hbm, cut), (ksq_hbm, ksq), (fwd_hbm, fwd), (inv_hbm, inv)]
-    local = [pltpu.make_async_copy(src, dst, in_sem.at[i]) for i, (src, dst) in enumerate(pairs)]
-    h_in, small_in, c_in, z_in, rest_in = local[0:4], local[4:7], local[7], local[8], local[9:]
-    for copy in h_in + small_in + [c_in]:
+    order = (2, 3, 0, 1)
+
+    def fetch(src, dst, i):
+        return pltpu.make_async_copy(src, dst, in_sem.at[i])
+
+    h_in = {r: fetch(h_hbm.at[r], h.at[r], i) for i, r in enumerate(order)}
+    c_in = fetch(c_hbm, c, 4)
+    small_in = [fetch(rates_hbm, rates, 5), fetch(thr_hbm, thr, 6), fetch(scal_hbm, scal, 7)]
+    z_in = fetch(z_hbm, z, 0)
+    tables_in = [fetch(fwd_hbm, fwd, 1), fetch(inv_hbm, inv, 2)]
+    factor_in = [fetch(flags_hbm, flags, 5), fetch(cut_hbm, cut, 6), fetch(ksq_hbm, ksq, 7)]
+    for copy in small_in + [h_in[r] for r in order] + [c_in]:
         copy.start()
 
     last = total - 1
@@ -168,28 +173,32 @@
     def _():
         signal(low_in, along(1))
 
+    def landed(ref, sem):
+        pltpu.make_async_copy(ref, ref, sem).wait()
+
     def halo_copy(side, field):
         step, h_row, c_row = ((1, rows - 2, rows - 1), (-1, 0, 0))[side]
-        src = (h.at[pl.ds(h_row, 2)], c.at[c_row])[field]
-        dst = (halo_h.at[side], halo_c.at[side])[field]
+        src = (h.at[pl.ds(h_row, 2)], c.at[pl.ds(c_row, 1)])[field]
+        dst = halo.at[side, pl.ds((0, 2)[field], (2, 1)[field])]
         return pltpu.make_async_remote_copy(
-            src, dst, halo_send.at[side, field], halo_recv.at[side, field], device_id=along(step), device_id_type=MESH
+            src, dst, halo_send.at[side], halo_recv.at[side], device_id=along(step), device_id_type=MESH
         )
 
     base[:, :, nlon:] = jnp.zeros((rows, levels, base.shape[2] - nlon), jnp.float32)
 
     @pl.when(position == 0)
     def _():
-        halo_h[0] = jnp.zeros_like(halo_h[0])
-        halo_c[0] = jnp.zeros_like(halo_c[0])
+        halo[0] = jnp.zeros_like(halo[0])
 
     @pl.when(position == last)
     def _():
-        halo_h[1] = jnp.zeros_like(halo_h[1])
-        halo_c[1] = jnp.zeros_like(halo_c[1])
-
-    for copy in small_in + h_in:
+        halo[1] = jnp.zeros_like(halo[1])
+
+    for copy in small_in:
         copy.wait()
+
+    h_in[2].wait()
+    h_in[3].wait()
 
     @pl.when(core == 0)
     def _():
@@ -206,36 +215,43 @@
         return value
 
     full = nlon // HALF
-    for g in range(levels // 8):
-        lev = pl.ds(8 * g, 8)
-        rate, threshold = levels_of(rates, 8 * g), levels_of(thr, 8 * g)
-        wide, rest = 0.0, 0.0
-        for r in range(rows):
+    groups = range(levels // 8)
+    rate_of = [levels_of(rates, 8 * g) for g in groups]
+    threshold_of = [levels_of(thr, 8 * g) for g in groups]
+    wide, rest = [0.0 for g in groups], [0.0 for g in groups]
+    for r in order:
+        if r < 2:
+            h_in[r].wait()
+        for g in groups:
+            lev = pl.ds(8 * g, 8)
             positive, factors = 0.0, 1.0
             for j in range(full):
-                s = h[r, lev, HALF * j : HALF * (j + 1)] - threshold
+                s = h[r, lev, HALF * j : HALF * (j + 1)] - threshold_of[g]
                 positive = positive + jnp.maximum(s, 0.0)
                 factors = factors * (1.0 + jnp.exp(-jnp.abs(s)))
-            s = h[r, lev, HALF * full : nlon] - threshold
-            wide = wide + scal[first + r] * (positive + jnp.log(factors))
-            rest = rest + scal[first + r] * (jnp.maximum(s, 0.0) + jnp.log(1.0 + jnp.exp(-jnp.abs(s))))
-        sums = jnp.sum(wide, axis=1, keepdims=True) + jnp.sum(rest, axis=1, keepdims=True)
-        tile = jnp.where(lane == g, -rate * sums, tile)
-        level_rates[g], level_thresholds[g] = jnp.broadcast_to(rate, (8, HALF)), jnp.broadcast_to(threshold, (8, HALF))
+            s = h[r, lev, HALF * full : nlon] - threshold_of[g]
+            wide[g] = wide[g] + scal[first + r] * (positive + jnp.log(factors))
+            rest[g] = rest[g] + scal[first + r] * (jnp.maximum(s, 0.0) + jnp.log(1.0 + jnp.exp(-jnp.abs(s))))
+    short = jnp.zeros((8, HALF * (full + 1) - nlon), jnp.float32)
+    for g in groups:
+        sums = jnp.sum(wide[g] + jnp.concatenate([rest[g], short], axis=1), axis=1, keepdims=True)
+        tile = jnp.where(lane == g, -rate_of[g] * sums, tile)
+        level_rates[g] = jnp.broadcast_to(rate_of[g], (8, HALF))
+        level_thresholds[g] = jnp.broadcast_to(threshold_of[g], (8, HALF))
     part[...] = tile
 
     def part_copy(slot):
         return pltpu.make_async_remote_copy(
-            part, xbuf.at[slot], x_send, x_recv.at[slot], device_id=row(1), device_id_type=MESH
+            part, box.at[slot], up_send, x_recv, device_id=row(1), device_id_type=MESH
         )
 
     @pl.when(jnp.logical_not(is_root))
     def _():
         part_copy(x * NC + core).start()
 
-    for copy in [z_in] + rest_in:
+    c_in.wait()
+    for copy in [z_in] + factor_in + tables_in:
         copy.start()
-    c_in.wait()
 
     @pl.when(jnp.logical_and(core != 0, position < last))
     def _():
@@ -290,46 +306,42 @@
         halo_copy(1, 0).start()
         halo_copy(1, 1).start()
 
-    for copy in rest_in[0:3]:
+    for copy in factor_in:
         copy.wait()
     for r in range(rows):
         cutoff = cut[first + r].astype(jnp.float32)
         flag = flags[first + r].astype(jnp.float32)
         factor[r] = flag * (1.0 - jnp.minimum(1.0, cutoff * cutoff * ksq[...]))
 
-    def landed(ref, sem):
-        pltpu.make_async_copy(ref, ref, sem).wait()
-
     def sum_copy():
         return pltpu.make_async_remote_copy(
-            ysum, ybuf.at[y], y_send, y_recv.at[y], device_id=root(0), device_id_type=MESH
+            part, box.at[NX * NC + y], up_send, y_recv, device_id=root(0), device_id_type=MESH
         )
 
-    def mean_copy(slot, device):
+    def mean_copy(device):
         return pltpu.make_async_remote_copy(
-            mean_in, mean_in, mean_send.at[slot], mean_recv, device_id=device, device_id_type=MESH
+            mean_in, mean_in, mean_send, mean_recv, device_id=device, device_id_type=MESH
         )
 
-    members = [0] + [k for d in (4, 3, 5, 2, 6, 1, 7) for k in (NC * d, NC * d + 1)]
+    members = [k for d in (4, 3, 5, 2, 6, 1, 7) for k in (NC * d, NC * d + 1)] + [0]
 
     def gather_row():
-        for k in members:
-            landed(xbuf.at[k], x_recv.at[k])
+        landed(box.at[pl.ds(0, len(members))], x_recv)
         acc = part[...]
         for k in members:
-            acc = acc + xbuf[k]
+            acc = acc + box[k]
         return acc
 
     def spread_row():
-        for k in members[1:] + members[:1]:
-            mean_copy(k, row(k)).start()
+        for k in members:
+            mean_copy(row(k)).start()
 
     @pl.when(is_later_root)
     def _():
-        ysum[...] = gather_row()
+        part[...] = gather_row()
         sum_copy().start()
 
-    for copy in rest_in[3:]:
+    for copy in tables_in:
         copy.wait()
     lanes = lax.broadcasted_iota(jnp.int32, (16, HALF), 1)
     units = 2 * levels
@@ -337,18 +349,18 @@
 
     def edges_above(g, carry):
         lev = pl.ds(pl.multiple_of(8 * g, 8), 8)
-        above, above2 = halo_h[1, 0, lev, :], halo_h[1, 1, lev, :]
+        above, above2 = halo[1, 0, lev, :], halo[1, 1, lev, :]
         t3 = s_hi[lev, :] * above
-        f4 = face(4) * (halo_c[1, lev, :] + c[3, lev, :]) * (7.0 * (above + h[3, lev, :]) - (above2 + h[2, lev, :]))
+        f4 = face(4) * (halo[1, 2, lev, :] + c[3, lev, :]) * (7.0 * (above + h[3, lev, :]) - (above2 + h[2, lev, :]))
         base[2, lev, 0:nlon] = base[2, lev, 0:nlon] + t3 * inv_cos(2)
         base[3, lev, 0:nlon] = base[3, lev, 0:nlon] - (t3 + f4) * inv_cos(3)
         return carry
 
     def edges_below(g, carry):
         lev = pl.ds(pl.multiple_of(8 * g, 8), 8)
-        below, below2 = halo_h[0, 1, lev, :], halo_h[0, 0, lev, :]
+        below, below2 = halo[0, 1, lev, :], halo[0, 0, lev, :]
         t1 = s_lo[lev, :] * below
-        f0 = face(0) * (halo_c[0, lev, :] + c[0, lev, :]) * (7.0 * (below + h[0, lev, :]) - (below2 + h[1, lev, :]))
+        f0 = face(0) * (halo[0, 2, lev, :] + c[0, lev, :]) * (7.0 * (below + h[0, lev, :]) - (below2 + h[1, lev, :]))
         base[0, lev, 0:nlon] = base[0, lev, 0:nlon] + (t1 + f0) * inv_cos(0)
         base[1, lev, 0:nlon] = base[1, lev, 0:nlon] - t1 * inv_cos(1)
         return carry
@@ -406,35 +418,32 @@
 
     @pl.when(position < last)
     def _():
-        halo_copy(1, 0).wait_recv()
-        halo_copy(1, 1).wait_recv()
+        landed(halo.at[1], halo_recv.at[1])
 
     lax.fori_loop(0, levels // 8, edges_above, 0)
     filter_rows(2)
 
     @pl.when(is_first)
     def _():
-        for k in range(1, NY):
-            landed(ybuf.at[k], y_recv.at[k])
-        acc = ybuf[1]
+        landed(box.at[pl.ds(NX * NC + 1, NY - 1)], y_recv)
+        acc = box[NX * NC + 1]
         for k in range(2, NY):
-            acc = acc + ybuf[k]
+            acc = acc + box[NX * NC + k]
         mean_in[...] = (gather_row() + acc) * (1.0 / area)
+        for k in (1, 4, 3, 5, 2, 6, 7):
+            mean_copy(root(k)).start()
         spread_row()
-        for k in range(1, NY):
-            mean_copy(NX * NC + k, root(k)).start()
 
     @pl.when(position > 0)
     def _():
-        halo_copy(0, 0).wait_recv()
-        halo_copy(0, 1).wait_recv()
+        landed(halo.at[0], halo_recv.at[0])
 
     lax.fori_loop(0, levels // 8, edges_below, 0)
     filter_rows(0)
 
     @pl.when(jnp.logical_not(is_first))
     def _():
-        mean_copy(0, row(0)).wait_recv()
+        landed(mean_in, mean_recv)
 
     @pl.when(is_later_root)
     def _():
@@ -450,26 +459,19 @@
 
         @pl.when(sender)
         def _():
-            halo_copy(side, 0).wait_send()
-            halo_copy(side, 1).wait_send()
+            landed(halo.at[side], halo_send.at[side])
+
+    @pl.when(is_first)
+    def _():
+        landed(box.at[pl.ds(0, len(members) + NY - 1)], mean_send)
 
     @pl.when(is_later_root)
     def _():
-        sum_copy().wait_send()
-
-    @pl.when(is_root)
-    def _():
-        for k in members:
-            mean_copy(k, row(k)).wait_send()
-
-    @pl.when(is_first)
-    def _():
-        for k in range(1, NY):
-            mean_copy(NX * NC + k, root(k)).wait_send()
-
-    @pl.when(jnp.logical_not(is_root))
-    def _():
-        part_copy(x * NC + core).wait_send()
+        landed(box.at[pl.ds(0, len(members))], mean_send)
+
+    @pl.when(jnp.logical_not(is_first))
+    def _():
+        landed(part, up_send)
 
 
 def local(height, zonal, merid, rates, thresholds, flags, cutoffs):
@@ -493,13 +495,12 @@
             smem(rates.shape, f32), smem(thresholds.shape, f32), smem(flags.shape, jnp.int32),
             smem(cutoffs.shape, jnp.int32), smem(scalars.shape, f32),
             vmem(ksq.shape, f32), vmem(fwd.shape, bf16), vmem(inv.shape, bf16),
-            vmem((2, 2, levels, nlon), f32), vmem((2, levels, nlon), f32), vmem((rows, levels, RADIX * HALF), f32),
+            vmem((2, 3, levels, nlon), f32), vmem((rows, levels, RADIX * HALF), f32),
             vmem((levels, nlon), f32), vmem((levels, nlon), f32), vmem((rows, 8, 2 * HALF), f32),
             vmem((tiles, 4 * levels, 2 * HALF), bf16), vmem((tiles, 2 * levels, 2 * HALF), f32),
-            vmem((8, HALF), f32), vmem((NX * NC, 8, HALF), f32), vmem((8, HALF), f32), vmem((NY, 8, HALF), f32),
-            vmem((8, HALF), f32), vmem((levels // 8, 8, HALF), f32), vmem((levels // 8, 8, HALF), f32),
-            dma((14,)), dma((2, 2)), dma((2, 2)),
-            dma, dma((NX * NC,)), dma, dma((NY,)), dma((NX * NC + NY,)), dma, pltpu.SemaphoreType.REGULAR,
+            vmem((8, HALF), f32), vmem((NX * NC + NY, 8, HALF), f32), vmem((8, HALF), f32),
+            vmem((levels // 8, 8, HALF), f32), vmem((levels // 8, 8, HALF), f32),
+            dma((8,)), dma((2,)), dma((2,)), dma, dma, dma, dma, dma, pltpu.SemaphoreType.REGULAR,
         ],
         compiler_params=pltpu.CompilerParams(collective_id=0, has_side_effects=True, vmem_limit_bytes=16 * 2**20),
         name="advect_filter",

time: 26.3 us -> 25.5 us (0.970)
  Pallas kernels: 25.3 us -> 24.5 us
    pallas_call x1, Pallas kernels: 25.3 us -> 24.5 us  [local(): pl.pallas_call(functools.partial(kernel, dims, nlon * cos_sum), out_shape...]
where the time goes in v5:
time: 25.5 us; the launch traced here: 25.4 us
  Pallas kernels  24.5 us (96%)
  local copies, waits for them, and re-layouts  0.88 us (3%)
    pallas_call x1, Pallas kernels, local(): pl.pallas_call(functools.partial(kernel, dims, nlon * cos_sum), out_shape...  24.5 us
    unnamed x1, local copies, waits for them, and re-layouts  0.88 us

profile of v5, /device:TPU:513, one launch (start us, length us, event | category | flops | bytes accessed | tf_op | source)
XLA Modules:
  0.0 25.4 jit_solution(855840666884890605)
XLA Ops:
  0.0 24.5 %advect_filter.1 = f32[4,32,1440]{2,1,0:T(8,128)S(1)} custom-call(f32[4,32,1440]{2,1,0:T(8,128)} %h_hbm.1, f32[4,32,1440]{2,1,0:T(8,128)} %z_hbm.1, f32[4,32,1440]{2,1,0:T(8,128)} %c_hbm.1, f32[32]{0:T(128)} %rates_hbm.1, f32[32]{0:T(128)} %thr_hbm.1, s32[512]{0:T(512)} %flags_hbm.1, s32[512]{0:T(512)} %cut_hbm.1, f32[1664]{0:T(1024)} %constant.8.clone.scal_hbm, ...), custom_call_target="tpu_custom_call" | custom-call | tf_op jit(solution)/shard_map/advect_filter/pallas_call | solution.py:488
  24.5 0.9 %copy.13 = f32[4,32,1440]{2,1,0:T(8,128)} copy(f32[4,32,1440]{2,1,0:T(8,128)S(1)} %advect_filter.1) | data formatting | bytes 1474560

commit v6 on v5

--- a/solution.py
+++ b/solution.py
@@ -107,7 +107,7 @@
     h_hbm, z_hbm, c_hbm, rates_hbm, thr_hbm, flags_hbm, cut_hbm, scal_hbm, ksq_hbm, fwd_hbm, inv_hbm,
     out,
     h, z, c, rates, thr, flags, cut, scal, ksq, fwd, inv,
-    halo, base, s_lo, s_hi, factor, ymat, wmat, part, box, mean_in, level_rates, level_thresholds,
+    halo, base, s_lo, s_hi, factor, ymat, wmat, part, box, mean_in, own_mean, level_rates, level_thresholds,
     in_sem, halo_send, halo_recv, up_send, x_recv, y_recv, mean_send, mean_recv, low_in,
 ):
     rows, levels, nlon, nlat = dims
@@ -122,12 +122,13 @@
         return pltpu.make_async_copy(src, dst, in_sem.at[i])
 
     h_in = {r: fetch(h_hbm.at[r], h.at[r], i) for i, r in enumerate(order)}
-    c_in = fetch(c_hbm, c, 4)
+    c_up = fetch(c_hbm.at[rows - 1], c.at[rows - 1], 4)
+    c_in = fetch(c_hbm.at[pl.ds(0, rows - 1)], c.at[pl.ds(0, rows - 1)], 3)
     small_in = [fetch(rates_hbm, rates, 5), fetch(thr_hbm, thr, 6), fetch(scal_hbm, scal, 7)]
     z_in = fetch(z_hbm, z, 0)
     tables_in = [fetch(fwd_hbm, fwd, 1), fetch(inv_hbm, inv, 2)]
     factor_in = [fetch(flags_hbm, flags, 5), fetch(cut_hbm, cut, 6), fetch(ksq_hbm, ksq, 7)]
-    for copy in small_in + [h_in[r] for r in order] + [c_in]:
+    for copy in small_in + [h_in[r] for r in order] + [c_up]:
         copy.start()
 
     last = total - 1
@@ -184,6 +185,7 @@
             src, dst, halo_send.at[side], halo_recv.at[side], device_id=along(step), device_id_type=MESH
         )
 
+    own_mean[...] = jnp.zeros_like(own_mean)
     base[:, :, nlon:] = jnp.zeros((rows, levels, base.shape[2] - nlon), jnp.float32)
 
     @pl.when(position == 0)
@@ -249,18 +251,20 @@
     def _():
         part_copy(x * NC + core).start()
 
+    c_up.wait()
+
+    @pl.when(jnp.logical_and(core != 0, position < last))
+    def _():
+        halo_copy(0, 0).start()
+
+    @pl.when(position < last)
+    def _():
+        halo_copy(0, 1).start()
+
+    for copy in [c_in, z_in] + factor_in + tables_in:
+        copy.start()
+
     c_in.wait()
-    for copy in [z_in] + factor_in + tables_in:
-        copy.start()
-
-    @pl.when(jnp.logical_and(core != 0, position < last))
-    def _():
-        halo_copy(0, 0).start()
-
-    @pl.when(position < last)
-    def _():
-        halo_copy(0, 1).start()
-
     z_in.wait()
 
     def inv_cos(r):
@@ -320,7 +324,7 @@
 
     def mean_copy(device):
         return pltpu.make_async_remote_copy(
-            mean_in, mean_in, mean_send, mean_recv, device_id=device, device_id_type=MESH
+            own_mean, mean_in, mean_send, mean_recv, device_id=device, device_id_type=MESH
         )
 
     members = [k for d in (4, 3, 5, 2, 6, 1, 7) for k in (NC * d, NC * d + 1)] + [0]
@@ -347,36 +351,42 @@
     units = 2 * levels
     blocks = levels // 16
 
-    def edges_above(g, carry):
-        lev = pl.ds(pl.multiple_of(8 * g, 8), 8)
-        above, above2 = halo[1, 0, lev, :], halo[1, 1, lev, :]
-        t3 = s_hi[lev, :] * above
-        f4 = face(4) * (halo[1, 2, lev, :] + c[3, lev, :]) * (7.0 * (above + h[3, lev, :]) - (above2 + h[2, lev, :]))
-        base[2, lev, 0:nlon] = base[2, lev, 0:nlon] + t3 * inv_cos(2)
-        base[3, lev, 0:nlon] = base[3, lev, 0:nlon] - (t3 + f4) * inv_cos(3)
-        return carry
-
-    def edges_below(g, carry):
-        lev = pl.ds(pl.multiple_of(8 * g, 8), 8)
-        below, below2 = halo[0, 1, lev, :], halo[0, 0, lev, :]
-        t1 = s_lo[lev, :] * below
-        f0 = face(0) * (halo[0, 2, lev, :] + c[0, lev, :]) * (7.0 * (below + h[0, lev, :]) - (below2 + h[1, lev, :]))
-        base[0, lev, 0:nlon] = base[0, lev, 0:nlon] + (t1 + f0) * inv_cos(0)
-        base[1, lev, 0:nlon] = base[1, lev, 0:nlon] - t1 * inv_cos(1)
-        return carry
+    tail = nlon - HALF * (RADIX - 1)
+
+    def piece(ref, j):
+        if j < RADIX - 1:
+            return ref[:, HALF * j : HALF * (j + 1)]
+        return jnp.concatenate([ref[:, HALF * j : nlon], jnp.zeros((16, HALF - tail), jnp.float32)], axis=1)
+
+    def with_halo(r, lev, j):
+        side, near, far, edge, inner, f, through, outer = (
+            (0, 1, 0, 0, 1, 0, s_lo, 0) if r < 2 else (1, 0, 1, rows - 1, rows - 2, rows, s_hi, rows - 1)
+        )
+        beside = piece(halo.at[side, near, lev], j)
+        term = piece(through.at[lev], j) * beside
+        if r == outer:
+            speed = face(f) * (piece(halo.at[side, 2, lev], j) + piece(c.at[edge, lev], j))
+            flux = speed * (
+                7.0 * (beside + piece(h.at[edge, lev], j)) - (piece(halo.at[side, far, lev], j) + piece(h.at[inner, lev], j))
+            )
+            term = term + flux
+        sign = 1.0 if r in (0, 2) else -1.0
+        return base[r, lev, HALF * j : HALF * (j + 1)] + term * (sign * inv_cos(r))
 
     def product(hilo, table):
         first_part = jnp.dot(hilo, table[0], preferred_element_type=jnp.float32)
         second = jnp.dot(hilo[0:units], table[1], preferred_element_type=jnp.float32)
         return first_part[0:units] + first_part[units : 2 * units] + second
 
-    def filter_rows(row0):
+    def filter_rows(row0, shifts=None):
         def block_of(b):
             return row0 + b // blocks, pl.ds(16 * (b % blocks), 16), pl.ds(16 * b, 16), pl.ds(units + 16 * b, 16)
 
         def forward(b):
             r, lev, at_hi, at_lo = block_of(b)
-            v = [base[r, lev, HALF * j : HALF * (j + 1)] for j in range(RADIX)]
+            v = [with_halo(r, lev, j) for j in range(RADIX)]
+            for j in range(RADIX):
+                base[r, lev, HALF * j : HALF * (j + 1)] = v[j]
             u = [v[0]] + [
                 pltpu.roll(jnp.where(lanes >= HALF - 8 * j, v[j - 1], v[j]), 8 * j, axis=1) for j in range(1, RADIX)
             ]
@@ -398,12 +408,13 @@
             removed += [even[RADIX - j] - odd[RADIX - j - 1] for j in range(7, RADIX)]
             back = [removed[0]] + [pltpu.roll(removed[j], HALF - 8 * j, axis=1) for j in range(1, RADIX)]
             for j in range(RADIX):
+                kept = base[r, lev, HALF * j : HALF * (j + 1)]
+                if row0 == 0:
+                    kept = kept - shifts[b % blocks]
                 if j < RADIX - 1:
-                    piece = jnp.where(lanes < count - 8 * j, back[j], back[j + 1])
-                    out[r, lev, HALF * j : HALF * (j + 1)] = base[r, lev, HALF * j : HALF * (j + 1)] - piece
+                    out[r, lev, HALF * j : HALF * (j + 1)] = kept - jnp.where(lanes < count - 8 * j, back[j], back[j + 1])
                 else:
-                    left = base[r, lev, HALF * j : HALF * (j + 1)] - back[j]
-                    out[r, lev, HALF * j : nlon] = left[:, 0 : nlon - HALF * j]
+                    out[r, lev, HALF * j : nlon] = (kept - back[j])[:, 0:tail]
 
         for b in range(2 * blocks):
             forward(b)
@@ -413,6 +424,11 @@
                 [waves[r * levels : (r + 1) * levels] * factor[row0 + r, m : m + 1, :] for r in range(2)], axis=0
             )
             wmat[m] = product(jnp.concatenate(split(scaled), axis=0), (inv[0, m], inv[1, m]))
+        if row0 == 0:
+            for r in (2, 3):
+                for b in range(blocks):
+                    lev = pl.ds(16 * b, 16)
+                    out[r, lev, :] = out[r, lev, :] - shifts[b]
         for b in range(2 * blocks):
             backward(b)
 
@@ -420,7 +436,6 @@
     def _():
         landed(halo.at[1], halo_recv.at[1])
 
-    lax.fori_loop(0, levels // 8, edges_above, 0)
     filter_rows(2)
 
     @pl.when(is_first)
@@ -429,7 +444,7 @@
         acc = box[NX * NC + 1]
         for k in range(2, NY):
             acc = acc + box[NX * NC + k]
-        mean_in[...] = (gather_row() + acc) * (1.0 / area)
+        own_mean[...] = (gather_row() + acc) * (1.0 / area)
         for k in (1, 4, 3, 5, 2, 6, 7):
             mean_copy(root(k)).start()
         spread_row()
@@ -438,8 +453,12 @@
     def _():
         landed(halo.at[0], halo_recv.at[0])
 
-    lax.fori_loop(0, levels // 8, edges_below, 0)
-    filter_rows(0)
+    def mean_columns(ref):
+        return [jnp.sum(jnp.where(lane == g, ref[...], 0.0), axis=1, keepdims=True) for g in groups]
+
+    columns = mean_columns(own_mean)
+    shifts = [jnp.concatenate(columns[2 * b : 2 * b + 2], axis=0) for b in range(blocks)]
+    filter_rows(0, shifts)
 
     @pl.when(jnp.logical_not(is_first))
     def _():
@@ -447,13 +466,15 @@
 
     @pl.when(is_later_root)
     def _():
+        own_mean[...] = mean_in[...]
         spread_row()
 
-    for g in range(levels // 8):
-        lev = pl.ds(8 * g, 8)
-        shift = jnp.sum(jnp.where(lane == g, mean_in[...], 0.0), axis=1, keepdims=True)
-        for r in range(rows):
-            out[r, lev, :] = out[r, lev, :] - shift
+    @pl.when(jnp.logical_not(is_first))
+    def _():
+        for g, shift in zip(groups, mean_columns(mean_in)):
+            lev = pl.ds(8 * g, 8)
+            for r in range(rows):
+                out[r, lev, :] = out[r, lev, :] - shift
 
     for side, sender in ((0, position < last), (1, position > 0)):
 
@@ -499,6 +520,7 @@
             vmem((levels, nlon), f32), vmem((levels, nlon), f32), vmem((rows, 8, 2 * HALF), f32),
             vmem((tiles, 4 * levels, 2 * HALF), bf16), vmem((tiles, 2 * levels, 2 * HALF), f32),
             vmem((8, HALF), f32), vmem((NX * NC + NY, 8, HALF), f32), vmem((8, HALF), f32),
+            vmem((8, HALF), f32),
             vmem((levels // 8, 8, HALF), f32), vmem((levels // 8, 8, HALF), f32),
             dma((8,)), dma((2,)), dma((2,)), dma, dma, dma, dma, dma, pltpu.SemaphoreType.REGULAR,
         ],

time: 25.5 us -> 25.3 us (level)
  no operation moved by 1% of the time
where the time goes in v6:
time: 25.3 us; the launch traced here: 25.2 us
  Pallas kernels  24.3 us (96%)
  local copies, waits for them, and re-layouts  0.88 us (3%)
    pallas_call x1, Pallas kernels, local(): pl.pallas_call(functools.partial(kernel, dims, nlon * cos_sum), out_shape...  24.3 us
    unnamed x1, local copies, waits for them, and re-layouts  0.88 us

profile of v6, /device:TPU:513, one launch (start us, length us, event | category | flops | bytes accessed | tf_op | source)
XLA Modules:
  0.0 25.2 jit_solution(46134268650435624)
XLA Ops:
  0.0 24.3 %advect_filter.1 = f32[4,32,1440]{2,1,0:T(8,128)S(1)} custom-call(f32[4,32,1440]{2,1,0:T(8,128)} %h_hbm.1, f32[4,32,1440]{2,1,0:T(8,128)} %z_hbm.1, f32[4,32,1440]{2,1,0:T(8,128)} %c_hbm.1, f32[32]{0:T(128)} %rates_hbm.1, f32[32]{0:T(128)} %thr_hbm.1, s32[512]{0:T(512)} %flags_hbm.1, s32[512]{0:T(512)} %cut_hbm.1, f32[1664]{0:T(1024)} %constant.8.clone.scal_hbm, ...), custom_call_target="tpu_custom_call" | custom-call | tf_op jit(solution)/shard_map/advect_filter/pallas_call | solution.py:509
  24.3 0.9 %copy.13 = f32[4,32,1440]{2,1,0:T(8,128)} copy(f32[4,32,1440]{2,1,0:T(8,128)S(1)} %advect_filter.1) | data formatting | bytes 1474560

commit v7 on v6

--- a/solution.py
+++ b/solution.py
@@ -15,6 +15,7 @@
 RADIX = 12
 HALF = 128
 ROOT = math.sqrt(0.75)
+LOG2E = math.log2(math.e)
 
 
 def filter_tables(nlon):
@@ -97,6 +98,13 @@
     return even, odd
 
 
+def product_of(exps):
+    result = 1.0 + exps[0]
+    for e in exps[1:]:
+        result = result * (1.0 + e)
+    return result
+
+
 def split(x):
     hi = x.astype(jnp.bfloat16)
     return hi, (x - hi.astype(jnp.float32)).astype(jnp.bfloat16)
@@ -179,10 +187,9 @@
 
     def halo_copy(side, field):
         step, h_row, c_row = ((1, rows - 2, rows - 1), (-1, 0, 0))[side]
-        src = (h.at[pl.ds(h_row, 2)], c.at[pl.ds(c_row, 1)])[field]
-        dst = halo.at[side, pl.ds((0, 2)[field], (2, 1)[field])]
+        src = c.at[c_row] if field == 2 else h.at[h_row + field]
         return pltpu.make_async_remote_copy(
-            src, dst, halo_send.at[side], halo_recv.at[side], device_id=along(step), device_id_type=MESH
+            src, halo.at[side, field], halo_send.at[side], halo_recv.at[side], device_id=along(step), device_id_type=MESH
         )
 
     own_mean[...] = jnp.zeros_like(own_mean)
@@ -199,12 +206,12 @@
     for copy in small_in:
         copy.wait()
 
-    h_in[2].wait()
-    h_in[3].wait()
-
-    @pl.when(core == 0)
-    def _():
-        halo_copy(0, 0).start()
+    for field in (0, 1):
+        h_in[rows - 2 + field].wait()
+
+        @pl.when(core == 0)
+        def _():
+            halo_copy(0, field).start()
 
     lane = lax.broadcasted_iota(jnp.int32, (8, HALF), 1)
     tile = jnp.zeros((8, HALF), jnp.float32)
@@ -220,24 +227,24 @@
     groups = range(levels // 8)
     rate_of = [levels_of(rates, 8 * g) for g in groups]
     threshold_of = [levels_of(thr, 8 * g) for g in groups]
+    scaled_threshold = [LOG2E * value for value in threshold_of]
     wide, rest = [0.0 for g in groups], [0.0 for g in groups]
     for r in order:
         if r < 2:
             h_in[r].wait()
         for g in groups:
             lev = pl.ds(8 * g, 8)
-            positive, factors = 0.0, 1.0
-            for j in range(full):
-                s = h[r, lev, HALF * j : HALF * (j + 1)] - threshold_of[g]
-                positive = positive + jnp.maximum(s, 0.0)
-                factors = factors * (1.0 + jnp.exp(-jnp.abs(s)))
-            s = h[r, lev, HALF * full : nlon] - threshold_of[g]
-            wide[g] = wide[g] + scal[first + r] * (positive + jnp.log(factors))
-            rest[g] = rest[g] + scal[first + r] * (jnp.maximum(s, 0.0) + jnp.log(1.0 + jnp.exp(-jnp.abs(s))))
+            exps = [
+                jnp.exp2(h[r, lev, HALF * j : HALF * (j + 1)] * LOG2E - scaled_threshold[g]) for j in range(full)
+            ]
+            logs = jnp.log2(product_of(exps[0:6])) + jnp.log2(product_of(exps[6:full]))
+            wide[g] = wide[g] + scal[first + r] * logs
+            logs = jnp.log2(1.0 + jnp.exp2(h[r, lev, HALF * full : nlon] * LOG2E - scaled_threshold[g]))
+            rest[g] = rest[g] + scal[first + r] * logs
     short = jnp.zeros((8, HALF * (full + 1) - nlon), jnp.float32)
     for g in groups:
         sums = jnp.sum(wide[g] + jnp.concatenate([rest[g], short], axis=1), axis=1, keepdims=True)
-        tile = jnp.where(lane == g, -rate_of[g] * sums, tile)
+        tile = jnp.where(lane == g, (-1.0 / LOG2E) * rate_of[g] * sums, tile)
         level_rates[g] = jnp.broadcast_to(rate_of[g], (8, HALF))
         level_thresholds[g] = jnp.broadcast_to(threshold_of[g], (8, HALF))
     part[...] = tile
@@ -256,10 +263,11 @@
     @pl.when(jnp.logical_and(core != 0, position < last))
     def _():
         halo_copy(0, 0).start()
+        halo_copy(0, 1).start()
 
     @pl.when(position < last)
     def _():
-        halo_copy(0, 1).start()
+        halo_copy(0, 2).start()
 
     for copy in [c_in, z_in] + factor_in + tables_in:
         copy.start()
@@ -298,7 +306,7 @@
             speed = zr + east(zr)
             flux = speed * (8.0 * pair - (west(pair) + east(pair))) * (1.0 / 24.0)
             s = hr[r] - threshold
-            source = rate * (jnp.maximum(s, 0.0) + jnp.log(1.0 + jnp.exp(-jnp.abs(s))))
+            source = rate * jnp.log(1.0 + jnp.exp(s))
             base[r, lev, 0:nlon] = (hr[r] - source) - (flux - west(flux)) - terms[r] * inv_cos(r)
         return carry
 
@@ -307,8 +315,8 @@
     @pl.when(position > 0)
     def _():
         pl.semaphore_wait(low_in, 1)
-        halo_copy(1, 0).start()
-        halo_copy(1, 1).start()
+        for field in range(3):
+            halo_copy(1, field).start()
 
     for copy in factor_in:
         copy.wait()
@@ -327,7 +335,7 @@
             own_mean, mean_in, mean_send, mean_recv, device_id=device, device_id_type=MESH
         )
 
-    members = [k for d in (4, 3, 5, 2, 6, 1, 7) for k in (NC * d, NC * d + 1)] + [0]
+    members = [*range(NC, NX * NC), 0]
 
     def gather_row():
         landed(box.at[pl.ds(0, len(members))], x_recv)
@@ -445,9 +453,11 @@
         for k in range(2, NY):
             acc = acc + box[NX * NC + k]
         own_mean[...] = (gather_row() + acc) * (1.0 / area)
-        for k in (1, 4, 3, 5, 2, 6, 7):
+        for k in range(1, NY):
             mean_copy(root(k)).start()
-        spread_row()
+            for member in members[2 * k - 2 : 2 * k]:
+                mean_copy(row(member)).start()
+        mean_copy(row(0)).start()
 
     @pl.when(position > 0)
     def _():

time: 25.3 us -> 25.2 us (level)
  no operation moved by 1% of the time
where the time goes in v7:
time: 25.2 us; the launch traced here: 25.1 us
  Pallas kernels  24.2 us (96%)
  local copies, waits for them, and re-layouts  0.88 us (3%)
    pallas_call x1, Pallas kernels, local(): pl.pallas_call(functools.partial(kernel, dims, nlon * cos_sum), out_shape...  24.2 us
    unnamed x1, local copies, waits for them, and re-layouts  0.88 us

profile of v7, /device:TPU:513, one launch (start us, length us, event | category | flops | bytes accessed | tf_op | source)
XLA Modules:
  0.0 25.1 jit_solution(10908787742789668187)
XLA Ops:
  0.0 24.2 %advect_filter.1 = f32[4,32,1440]{2,1,0:T(8,128)S(1)} custom-call(f32[4,32,1440]{2,1,0:T(8,128)} %h_hbm.1, f32[4,32,1440]{2,1,0:T(8,128)} %z_hbm.1, f32[4,32,1440]{2,1,0:T(8,128)} %c_hbm.1, f32[32]{0:T(128)} %rates_hbm.1, f32[32]{0:T(128)} %thr_hbm.1, s32[512]{0:T(512)} %flags_hbm.1, s32[512]{0:T(512)} %cut_hbm.1, f32[1664]{0:T(1024)} %constant.8.clone.scal_hbm, ...), custom_call_target="tpu_custom_call" | custom-call | tf_op jit(solution)/shard_map/advect_filter/pallas_call | solution.py:519
  24.2 0.9 %copy.13 = f32[4,32,1440]{2,1,0:T(8,128)} copy(f32[4,32,1440]{2,1,0:T(8,128)S(1)} %advect_filter.1) | data formatting | bytes 1474560

commit v8 on v7

--- a/solution.py
+++ b/solution.py
@@ -175,7 +175,14 @@
         for k in range(1, NY):
             signal(barrier, root(k))
 
+    to_start = jnp.logical_and(position > 1, jnp.logical_or(y == 0, is_root))
+
+    @pl.when(to_start)
+    def _():
+        signal(barrier, {"lat_0": jnp.int32(0), "lat_1": jnp.int32(0), "lat_2": jnp.int32(0)})
+
     greeted = jnp.where(is_first, 0, 1) + jnp.where(position < last, 1, 0)
+    greeted = greeted + jnp.where(position == 0, NX * NC - 2 + NY - 1, 0)
     pl.semaphore_wait(barrier, greeted)
 
     @pl.when(position < last)
@@ -185,14 +192,23 @@
     def landed(ref, sem):
         pltpu.make_async_copy(ref, ref, sem).wait()
 
-    def halo_copy(side, field):
+    def halo_copy(side, field, from_hbm=False):
         step, h_row, c_row = ((1, rows - 2, rows - 1), (-1, 0, 0))[side]
-        src = c.at[c_row] if field == 2 else h.at[h_row + field]
+        src = (c_hbm if from_hbm else c).at[c_row] if field == 2 else h.at[h_row + field]
         return pltpu.make_async_remote_copy(
             src, halo.at[side, field], halo_send.at[side], halo_recv.at[side], device_id=along(step), device_id_type=MESH
         )
 
+    @pl.when(core == 0)
+    def _():
+        halo_copy(0, 2, from_hbm=True).start()
+
     own_mean[...] = jnp.zeros_like(own_mean)
+
+    @pl.when(jnp.logical_and(y > 0, jnp.logical_not(is_root)))
+    def _():
+        mean_in[1] = jnp.zeros_like(mean_in[1])
+
     base[:, :, nlon:] = jnp.zeros((rows, levels, base.shape[2] - nlon), jnp.float32)
 
     @pl.when(position == 0)
@@ -249,31 +265,48 @@
         level_thresholds[g] = jnp.broadcast_to(threshold_of[g], (8, HALF))
     part[...] = tile
 
+    members = [*range(NC, NX * NC), 0]
+
+    def mean_copy(slot, source, device):
+        return pltpu.make_async_remote_copy(
+            source, mean_in.at[slot], mean_send, mean_recv, device_id=device, device_id_type=MESH
+        )
+
+    def send_b(device):
+        mean_copy(1, part, device).start()
+
     def part_copy(slot):
         return pltpu.make_async_remote_copy(
             part, box.at[slot], up_send, x_recv, device_id=row(1), device_id_type=MESH
         )
 
-    @pl.when(jnp.logical_not(is_root))
+    sends_part = jnp.logical_and(jnp.logical_not(is_root), position > 0)
+
+    @pl.when(sends_part)
     def _():
         part_copy(x * NC + core).start()
 
-    c_up.wait()
-
-    @pl.when(jnp.logical_and(core != 0, position < last))
-    def _():
-        halo_copy(0, 0).start()
-        halo_copy(0, 1).start()
-
-    @pl.when(position < last)
-    def _():
-        halo_copy(0, 2).start()
+    @pl.when(position == 0)
+    def _():
+        mean_in[1] = part[...]
+        send_b(row(1))
+        for k in range(1, NY):
+            for member in members[2 * k - 2 : 2 * k]:
+                send_b(row(member))
+            send_b(root(k))
 
     for copy in [c_in, z_in] + factor_in + tables_in:
         copy.start()
 
+    z_in.wait()
+    c_up.wait()
     c_in.wait()
-    z_in.wait()
+
+    @pl.when(jnp.logical_and(core != 0, position < last))
+    def _():
+        for field in range(3):
+            halo_copy(0, field).start()
+
 
     def inv_cos(r):
         return scal[nlat + first + r]
@@ -330,27 +363,16 @@
             part, box.at[NX * NC + y], up_send, y_recv, device_id=root(0), device_id_type=MESH
         )
 
-    def mean_copy(device):
-        return pltpu.make_async_remote_copy(
-            own_mean, mean_in, mean_send, mean_recv, device_id=device, device_id_type=MESH
-        )
-
-    members = [*range(NC, NX * NC), 0]
-
-    def gather_row():
-        landed(box.at[pl.ds(0, len(members))], x_recv)
+    def gather_row(senders):
+        landed(box.at[pl.ds(0, len(senders))], x_recv)
         acc = part[...]
-        for k in members:
+        for k in senders:
             acc = acc + box[k]
         return acc
 
-    def spread_row():
-        for k in members:
-            mean_copy(row(k)).start()
-
     @pl.when(is_later_root)
     def _():
-        part[...] = gather_row()
+        part[...] = gather_row(members)
         sum_copy().start()
 
     for copy in tables_in:
@@ -452,36 +474,48 @@
         acc = box[NX * NC + 1]
         for k in range(2, NY):
             acc = acc + box[NX * NC + k]
-        own_mean[...] = (gather_row() + acc) * (1.0 / area)
+        mean_in[0] = gather_row(members[:-1]) + acc
         for k in range(1, NY):
-            mean_copy(root(k)).start()
             for member in members[2 * k - 2 : 2 * k]:
-                mean_copy(row(member)).start()
-        mean_copy(row(0)).start()
+                mean_copy(0, mean_in.at[0], row(member)).start()
+            mean_copy(0, mean_in.at[0], root(k)).start()
+        mean_copy(0, mean_in.at[0], row(0)).start()
 
     @pl.when(position > 0)
     def _():
         landed(halo.at[0], halo_recv.at[0])
 
-    def mean_columns(ref):
-        return [jnp.sum(jnp.where(lane == g, ref[...], 0.0), axis=1, keepdims=True) for g in groups]
-
-    columns = mean_columns(own_mean)
+    @pl.when(is_first)
+    def _():
+        landed(mean_in.at[1], mean_recv)
+        own_mean[...] = (mean_in[0] + mean_in[1]) * (1.0 / area)
+
+    def mean_columns(value):
+        return [jnp.sum(jnp.where(lane == g, value, 0.0), axis=1, keepdims=True) for g in groups]
+
+    columns = mean_columns(own_mean[...])
     shifts = [jnp.concatenate(columns[2 * b : 2 * b + 2], axis=0) for b in range(blocks)]
     filter_rows(0, shifts)
 
+    in_two = jnp.logical_or(is_later_root, jnp.logical_and(y == 0, position > 1))
+
+    @pl.when(in_two)
+    def _():
+        landed(mean_in, mean_recv)
+
+    @pl.when(jnp.logical_not(jnp.logical_or(in_two, is_first)))
+    def _():
+        landed(mean_in.at[0], mean_recv)
+
+    @pl.when(is_later_root)
+    def _():
+        own_mean[...] = mean_in[0] + mean_in[1]
+        for member in members:
+            mean_copy(0, own_mean, row(member)).start()
+
     @pl.when(jnp.logical_not(is_first))
     def _():
-        landed(mean_in, mean_recv)
-
-    @pl.when(is_later_root)
-    def _():
-        own_mean[...] = mean_in[...]
-        spread_row()
-
-    @pl.when(jnp.logical_not(is_first))
-    def _():
-        for g, shift in zip(groups, mean_columns(mean_in)):
+        for g, shift in zip(groups, mean_columns((mean_in[0] + mean_in[1]) * (1.0 / area))):
             lev = pl.ds(8 * g, 8)
             for r in range(rows):
                 out[r, lev, :] = out[r, lev, :] - shift
@@ -492,7 +526,7 @@
         def _():
             landed(halo.at[side], halo_send.at[side])
 
-    @pl.when(is_first)
+    @pl.when(position <= 1)
     def _():
         landed(box.at[pl.ds(0, len(members) + NY - 1)], mean_send)
 
@@ -500,7 +534,7 @@
     def _():
         landed(box.at[pl.ds(0, len(members))], mean_send)
 
-    @pl.when(jnp.logical_not(is_first))
+    @pl.when(position > 1)
     def _():
         landed(part, up_send)
 
@@ -529,7 +563,7 @@
             vmem((2, 3, levels, nlon), f32), vmem((rows, levels, RADIX * HALF), f32),
             vmem((levels, nlon), f32), vmem((levels, nlon), f32), vmem((rows, 8, 2 * HALF), f32),
             vmem((tiles, 4 * levels, 2 * HALF), bf16), vmem((tiles, 2 * levels, 2 * HALF), f32),
-            vmem((8, HALF), f32), vmem((NX * NC + NY, 8, HALF), f32), vmem((8, HALF), f32),
+            vmem((8, HALF), f32), vmem((NX * NC + NY, 8, HALF), f32), vmem((2, 8, HALF), f32),
             vmem((8, HALF), f32),
             vmem((levels // 8, 8, HALF), f32), vmem((levels // 8, 8, HALF), f32),
             dma((8,)), dma((2,)), dma((2,)), dma, dma, dma, dma, dma, pltpu.SemaphoreType.REGULAR,

time: 25.2 us -> 25.8 us (1.024)
  Pallas kernels: 24.2 us -> 24.8 us
    pallas_call x1, Pallas kernels: 24.2 us -> 24.8 us  [local(): pl.pallas_call(functools.partial(kernel, dims, nlon * cos_sum), out_shape...]
where the time goes in v8:
time: 25.8 us; the launch traced here: 25.7 us
  Pallas kernels  24.8 us (96%)
  local copies, waits for them, and re-layouts  0.88 us (3%)
    pallas_call x1, Pallas kernels, local(): pl.pallas_call(functools.partial(kernel, dims, nlon * cos_sum), out_shape...  24.8 us
    unnamed x1, local copies, waits for them, and re-layouts  0.88 us

profile of v8, /device:TPU:513, one launch (start us, length us, event | category | flops | bytes accessed | tf_op | source)
XLA Modules:
  0.0 25.7 jit_solution(16722045104568135562)
XLA Ops:
  0.0 24.8 %advect_filter.1 = f32[4,32,1440]{2,1,0:T(8,128)S(1)} custom-call(f32[4,32,1440]{2,1,0:T(8,128)} %h_hbm.1, f32[4,32,1440]{2,1,0:T(8,128)} %z_hbm.1, f32[4,32,1440]{2,1,0:T(8,128)} %c_hbm.1, f32[32]{0:T(128)} %rates_hbm.1, f32[32]{0:T(128)} %thr_hbm.1, s32[512]{0:T(512)} %flags_hbm.1, s32[512]{0:T(512)} %cut_hbm.1, f32[1664]{0:T(1024)} %constant.8.clone.scal_hbm, ...), custom_call_target="tpu_custom_call" | custom-call | tf_op jit(solution)/shard_map/advect_filter/pallas_call | solution.py:553
  24.8 0.9 %copy.13 = f32[4,32,1440]{2,1,0:T(8,128)} copy(f32[4,32,1440]{2,1,0:T(8,128)S(1)} %advect_filter.1) | data formatting | bytes 1474560

commit v9 on v8

--- a/solution.py
+++ b/solution.py
@@ -12,6 +12,7 @@
 
 MESH = pl.DeviceIdType.MESH
 NX, NY, NC = 8, 8, 2
+PIECES = 2
 RADIX = 12
 HALF = 128
 ROOT = math.sqrt(0.75)
@@ -125,18 +126,23 @@
     total = NX * NY * NC
 
     order = (2, 3, 0, 1)
+    cut_at = levels // PIECES
+    pieces = [pl.ds(cut_at * i, cut_at) for i in range(PIECES)]
 
     def fetch(src, dst, i):
         return pltpu.make_async_copy(src, dst, in_sem.at[i])
 
-    h_in = {r: fetch(h_hbm.at[r], h.at[r], i) for i, r in enumerate(order)}
-    c_up = fetch(c_hbm.at[rows - 1], c.at[rows - 1], 4)
-    c_in = fetch(c_hbm.at[pl.ds(0, rows - 1)], c.at[pl.ds(0, rows - 1)], 3)
-    small_in = [fetch(rates_hbm, rates, 5), fetch(thr_hbm, thr, 6), fetch(scal_hbm, scal, 7)]
+    up_in = [[fetch(h_hbm.at[r, p], h.at[r, p], PIECES * (r - 2) + i) for i, p in enumerate(pieces)] for r in (2, 3)]
+    low_rows = fetch(h_hbm.at[pl.ds(0, 2)], h.at[pl.ds(0, 2)], 2 * PIECES)
+    c_up = fetch(c_hbm.at[rows - 1], c.at[rows - 1], 2 * PIECES + 1)
+    small_in = [fetch(src, dst, 2 * PIECES + 2 + i) for i, (src, dst) in enumerate(((rates_hbm, rates), (thr_hbm, thr), (scal_hbm, scal)))]
     z_in = fetch(z_hbm, z, 0)
+    c_in = fetch(c_hbm.at[pl.ds(0, rows - 1)], c.at[pl.ds(0, rows - 1)], 2 * PIECES)
     tables_in = [fetch(fwd_hbm, fwd, 1), fetch(inv_hbm, inv, 2)]
-    factor_in = [fetch(flags_hbm, flags, 5), fetch(cut_hbm, cut, 6), fetch(ksq_hbm, ksq, 7)]
-    for copy in small_in + [h_in[r] for r in order] + [c_up]:
+    factor_in = [
+        fetch(src, dst, 2 * PIECES + 2 + i) for i, (src, dst) in enumerate(((flags_hbm, flags), (cut_hbm, cut), (ksq_hbm, ksq)))
+    ]
+    for copy in small_in + up_in[0] + up_in[1] + [low_rows, c_up]:
         copy.start()
 
     last = total - 1
@@ -192,17 +198,14 @@
     def landed(ref, sem):
         pltpu.make_async_copy(ref, ref, sem).wait()
 
-    def halo_copy(side, field, from_hbm=False):
+    def halo_copy(side, field, levs=slice(None)):
         step, h_row, c_row = ((1, rows - 2, rows - 1), (-1, 0, 0))[side]
-        src = (c_hbm if from_hbm else c).at[c_row] if field == 2 else h.at[h_row + field]
+        src = c.at[c_row, levs] if field == 2 else h.at[h_row + field, levs]
         return pltpu.make_async_remote_copy(
-            src, halo.at[side, field], halo_send.at[side], halo_recv.at[side], device_id=along(step), device_id_type=MESH
+            src, halo.at[side, field, levs], halo_send.at[side], halo_recv.at[side],
+            device_id=along(step), device_id_type=MESH,
         )
 
-    @pl.when(core == 0)
-    def _():
-        halo_copy(0, 2, from_hbm=True).start()
-
     own_mean[...] = jnp.zeros_like(own_mean)
 
     @pl.when(jnp.logical_and(y > 0, jnp.logical_not(is_root)))
@@ -218,16 +221,17 @@
     @pl.when(position == last)
     def _():
         halo[1] = jnp.zeros_like(halo[1])
+
+    for field in (0, 1):
+        for arrived, levs in zip(up_in[field], pieces):
+            arrived.wait()
+
+            @pl.when(core == 0)
+            def _():
+                halo_copy(0, field, levs).start()
 
     for copy in small_in:
         copy.wait()
-
-    for field in (0, 1):
-        h_in[rows - 2 + field].wait()
-
-        @pl.when(core == 0)
-        def _():
-            halo_copy(0, field).start()
 
     lane = lax.broadcasted_iota(jnp.int32, (8, HALF), 1)
     tile = jnp.zeros((8, HALF), jnp.float32)
@@ -246,8 +250,8 @@
     scaled_threshold = [LOG2E * value for value in threshold_of]
     wide, rest = [0.0 for g in groups], [0.0 for g in groups]
     for r in order:
-        if r < 2:
-            h_in[r].wait()
+        if r == 0:
+            low_rows.wait()
         for g in groups:
             lev = pl.ds(8 * g, 8)
             exps = [
@@ -288,8 +292,22 @@
 
     @pl.when(position == 0)
     def _():
+        send_b(row(1))
+
+    c_up.wait()
+
+    @pl.when(jnp.logical_and(core != 0, position < last))
+    def _():
+        halo_copy(0, 0).start()
+        halo_copy(0, 1).start()
+
+    @pl.when(position < last)
+    def _():
+        halo_copy(0, 2).start()
+
+    @pl.when(position == 0)
+    def _():
         mean_in[1] = part[...]
-        send_b(row(1))
         for k in range(1, NY):
             for member in members[2 * k - 2 : 2 * k]:
                 send_b(row(member))
@@ -299,13 +317,7 @@
         copy.start()
 
     z_in.wait()
-    c_up.wait()
     c_in.wait()
-
-    @pl.when(jnp.logical_and(core != 0, position < last))
-    def _():
-        for field in range(3):
-            halo_copy(0, field).start()
 
 
     def inv_cos(r):
@@ -566,7 +578,7 @@
             vmem((8, HALF), f32), vmem((NX * NC + NY, 8, HALF), f32), vmem((2, 8, HALF), f32),
             vmem((8, HALF), f32),
             vmem((levels // 8, 8, HALF), f32), vmem((levels // 8, 8, HALF), f32),
-            dma((8,)), dma((2,)), dma((2,)), dma, dma, dma, dma, dma, pltpu.SemaphoreType.REGULAR,
+            dma((2 * PIECES + 5,)), dma((2,)), dma((2,)), dma, dma, dma, dma, dma, pltpu.SemaphoreType.REGULAR,
         ],
         compiler_params=pltpu.CompilerParams(collective_id=0, has_side_effects=True, vmem_limit_bytes=16 * 2**20),
         name="advect_filter",

time: 25.8 us -> 25.1 us (0.973)
  Pallas kernels: 24.8 us -> 24.1 us
    pallas_call x1, Pallas kernels: 24.8 us -> 24.1 us  [local(): pl.pallas_call(functools.partial(kernel, dims, nlon * cos_sum), out_shape...]
where the time goes in v9:
time: 25.1 us; the launch traced here: 25 us
  Pallas kernels  24.1 us (96%)
  local copies, waits for them, and re-layouts  0.88 us (4%)
    pallas_call x1, Pallas kernels, local(): pl.pallas_call(functools.partial(kernel, dims, nlon * cos_sum), out_shape...  24.1 us
    unnamed x1, local copies, waits for them, and re-layouts  0.88 us

profile of v9, /device:TPU:513, one launch (start us, length us, event | category | flops | bytes accessed | tf_op | source)
XLA Modules:
  0.0 25.0 jit_solution(11400121382796255253)
XLA Ops:
  0.0 24.1 %advect_filter.1 = f32[4,32,1440]{2,1,0:T(8,128)S(1)} custom-call(f32[4,32,1440]{2,1,0:T(8,128)} %h_hbm.1, f32[4,32,1440]{2,1,0:T(8,128)} %z_hbm.1, f32[4,32,1440]{2,1,0:T(8,128)} %c_hbm.1, f32[32]{0:T(128)} %rates_hbm.1, f32[32]{0:T(128)} %thr_hbm.1, s32[512]{0:T(512)} %flags_hbm.1, s32[512]{0:T(512)} %cut_hbm.1, f32[1664]{0:T(1024)} %constant.8.clone.scal_hbm, ...), custom_call_target="tpu_custom_call" | custom-call | tf_op jit(solution)/shard_map/advect_filter/pallas_call | solution.py:565
  24.1 0.9 %copy.13 = f32[4,32,1440]{2,1,0:T(8,128)} copy(f32[4,32,1440]{2,1,0:T(8,128)S(1)} %advect_filter.1) | data formatting | bytes 1474560

commit v10 on v9

--- a/solution.py
+++ b/solution.py
@@ -85,18 +85,33 @@
     return table.astype(np.float32), float(np.sum(cos_row))
 
 
-def twelve(e, o):
+def sums_of_twelve(e, o):
     plus, minus = e[0] + e[6], e[0] - e[6]
     e15p, e15m, e24p, e24m = e[1] + e[5], e[1] - e[5], e[2] + e[4], e[2] - e[4]
-    a, b = plus + e24p, e15p + e[3]
-    big, mid = ROOT * e15m, minus + 0.5 * e24m
-    c, d = plus - 0.5 * e24p, 0.5 * e15p - e[3]
-    even = [a + b, mid + big, c + d, minus - e24m, c - d, mid - big, a - b]
     o15p, o15m, o24p, o24m = o[0] + o[4], o[0] - o[4], o[1] + o[3], o[1] - o[3]
-    f, g = 0.5 * o15p + o[2], ROOT * o24p
-    s, t = ROOT * o15m, ROOT * o24m
-    odd = [f + g, s + t, o15p - o[2], s - t, f - g]
-    return even, odd
+    return [
+        plus + e24p, e15p + e[3], minus + 0.5 * e24m, ROOT * e15m, 0.5 * o15p + o[2], ROOT * o24p,
+        plus - 0.5 * e24p, 0.5 * e15p - e[3], ROOT * o15m, ROOT * o24m, minus - e24m, o15p - o[2],
+    ]
+
+
+CLASSES = {
+    0: ((0, 1, 1), (0, 1, -1)), 1: ((2, 3, 1), (4, 5, 1)), 5: ((2, 3, -1), (4, 5, -1)),
+    2: ((6, 7, 1), (8, 9, 1)), 4: ((6, 7, -1), (8, 9, -1)), 3: ((10, None, 1), (11, None, 1)),
+}
+
+
+def combine(sums, which):
+    i, j, sign = which
+    if j is None:
+        return sums(i)
+    return sums(i) + sums(j) if sign > 0 else sums(i) - sums(j)
+
+
+def twelve(e, o):
+    sums = sums_of_twelve(e, o)
+    parts = {m: [combine(lambda i: sums[i], which) for which in pair] for m, pair in CLASSES.items()}
+    return [parts[m][0] for m in range(6)] + [parts[0][1]], [parts[m][1] for m in range(1, 6)]
 
 
 def product_of(exps):
@@ -116,7 +131,7 @@
     h_hbm, z_hbm, c_hbm, rates_hbm, thr_hbm, flags_hbm, cut_hbm, scal_hbm, ksq_hbm, fwd_hbm, inv_hbm,
     out,
     h, z, c, rates, thr, flags, cut, scal, ksq, fwd, inv,
-    halo, base, s_lo, s_hi, factor, ymat, wmat, part, box, mean_in, own_mean, level_rates, level_thresholds,
+    halo, base, s_lo, s_hi, factor, mids, ymat, wmat, part, box, mean_in, own_mean, level_rates, level_thresholds,
     in_sem, halo_send, halo_recv, up_send, x_recv, y_recv, mean_send, mean_recv, low_in,
 ):
     rows, levels, nlon, nlat = dims
@@ -434,13 +449,15 @@
             ]
             e = [u[0]] + [u[j] + u[RADIX - j] for j in range(1, 6)] + [u[6]]
             o = [u[j] - u[RADIX - j] for j in range(1, 6)]
-            even, odd = twelve(e, o)
-            halves = [(even[0], even[6])] + [(even[m], odd[m - 1]) for m in range(1, 6)]
-            for m, pair in enumerate(halves):
-                for k, value in enumerate(pair):
-                    hi, lo = split(value)
-                    ymat[m, at_hi, HALF * k : HALF * (k + 1)] = hi
-                    ymat[m, at_lo, HALF * k : HALF * (k + 1)] = lo
+            for i, value in enumerate(sums_of_twelve(e, o)):
+                mids[i, at_hi, :] = value
+
+        def finish(m, b):
+            _, _, at_hi, at_lo = block_of(b)
+            for k, which in enumerate(CLASSES[m]):
+                hi, lo = split(combine(lambda i: mids[i, at_hi, :], which))
+                ymat[m, at_hi, HALF * k : HALF * (k + 1)] = hi
+                ymat[m, at_lo, HALF * k : HALF * (k + 1)] = lo
 
         def backward(b):
             r, lev, at, _ = block_of(b)
@@ -460,7 +477,9 @@
 
         for b in range(2 * blocks):
             forward(b)
-        for m in range(RADIX // 2):
+        for m in CLASSES:
+            for b in range(2 * blocks):
+                finish(m, b)
             waves = product(ymat[m], (fwd[0, m], fwd[1, m]))
             scaled = jnp.concatenate(
                 [waves[r * levels : (r + 1) * levels] * factor[row0 + r, m : m + 1, :] for r in range(2)], axis=0
@@ -574,7 +593,7 @@
             vmem(ksq.shape, f32), vmem(fwd.shape, bf16), vmem(inv.shape, bf16),
             vmem((2, 3, levels, nlon), f32), vmem((rows, levels, RADIX * HALF), f32),
             vmem((levels, nlon), f32), vmem((levels, nlon), f32), vmem((rows, 8, 2 * HALF), f32),
-            vmem((tiles, 4 * levels, 2 * HALF), bf16), vmem((tiles, 2 * levels, 2 * HALF), f32),
+            vmem((RADIX, 2 * levels, HALF), f32), vmem((tiles, 4 * levels, 2 * HALF), bf16), vmem((tiles, 2 * levels, 2 * HALF), f32),
             vmem((8, HALF), f32), vmem((NX * NC + NY, 8, HALF), f32), vmem((2, 8, HALF), f32),
             vmem((8, HALF), f32),
             vmem((levels // 8, 8, HALF), f32), vmem((levels // 8, 8, HALF), f32),

time: 25.1 us -> 25.1 us (level)
  no operation moved by 1% of the time
where the time goes in v10:
time: 25.1 us; the launch traced here: 25 us
  Pallas kernels  24.1 us (96%)
  local copies, waits for them, and re-layouts  0.88 us (4%)
    pallas_call x1, Pallas kernels, local(): pl.pallas_call(functools.partial(kernel, dims, nlon * cos_sum), out_shape...  24.1 us
    unnamed x1, local copies, waits for them, and re-layouts  0.88 us

profile of v10, /device:TPU:513, one launch (start us, length us, event | category | flops | bytes accessed | tf_op | source)
XLA Modules:
  0.0 25.0 jit_solution(4396626101866127177)
XLA Ops:
  0.0 24.1 %advect_filter.1 = f32[4,32,1440]{2,1,0:T(8,128)S(1)} custom-call(f32[4,32,1440]{2,1,0:T(8,128)} %h_hbm.1, f32[4,32,1440]{2,1,0:T(8,128)} %z_hbm.1, f32[4,32,1440]{2,1,0:T(8,128)} %c_hbm.1, f32[32]{0:T(128)} %rates_hbm.1, f32[32]{0:T(128)} %thr_hbm.1, s32[512]{0:T(512)} %flags_hbm.1, s32[512]{0:T(512)} %cut_hbm.1, f32[1664]{0:T(1024)} %constant.8.clone.scal_hbm, ...), custom_call_target="tpu_custom_call" | custom-call | tf_op jit(solution)/shard_map/advect_filter/pallas_call | solution.py:584
  24.1 0.9 %copy.13 = f32[4,32,1440]{2,1,0:T(8,128)} copy(f32[4,32,1440]{2,1,0:T(8,128)S(1)} %advect_filter.1) | data formatting | bytes 1474560

commit v11 on v9

--- a/solution.py
+++ b/solution.py
@@ -125,7 +125,7 @@
     position = (x * NY + y) * NC + core
     total = NX * NY * NC
 
-    order = (2, 3, 0, 1)
+    order = (3, 2, 0, 1)
     cut_at = levels // PIECES
     pieces = [pl.ds(cut_at * i, cut_at) for i in range(PIECES)]
 
@@ -142,7 +142,7 @@
     factor_in = [
         fetch(src, dst, 2 * PIECES + 2 + i) for i, (src, dst) in enumerate(((flags_hbm, flags), (cut_hbm, cut), (ksq_hbm, ksq)))
     ]
-    for copy in small_in + up_in[0] + up_in[1] + [low_rows, c_up]:
+    for copy in small_in + up_in[1] + up_in[0] + [low_rows, c_up]:
         copy.start()
 
     last = total - 1
@@ -202,7 +202,7 @@
         step, h_row, c_row = ((1, rows - 2, rows - 1), (-1, 0, 0))[side]
         src = c.at[c_row, levs] if field == 2 else h.at[h_row + field, levs]
         return pltpu.make_async_remote_copy(
-            src, halo.at[side, field, levs], halo_send.at[side], halo_recv.at[side],
+            src, halo.at[side, field, levs], halo_send.at[side], halo_recv.at[side, 0 if field == 1 - side else 1],
             device_id=along(step), device_id_type=MESH,
         )
 
@@ -222,7 +222,7 @@
     def _():
         halo[1] = jnp.zeros_like(halo[1])
 
-    for field in (0, 1):
+    for field in (1, 0):
         for arrived, levs in zip(up_in[field], pieces):
             arrived.wait()
 
@@ -298,8 +298,8 @@
 
     @pl.when(jnp.logical_and(core != 0, position < last))
     def _():
+        halo_copy(0, 1).start()
         halo_copy(0, 0).start()
-        halo_copy(0, 1).start()
 
     @pl.when(position < last)
     def _():
@@ -420,7 +420,10 @@
         second = jnp.dot(hilo[0:units], table[1], preferred_element_type=jnp.float32)
         return first_part[0:units] + first_part[units : 2 * units] + second
 
-    def filter_rows(row0, shifts=None):
+    def filter_rows(row0, side, between):
+        sender = position > 0 if side == 0 else position < last
+        outer = 0 if side == 0 else 1
+
         def block_of(b):
             return row0 + b // blocks, pl.ds(16 * (b % blocks), 16), pl.ds(16 * b, 16), pl.ds(units + 16 * b, 16)
 
@@ -458,8 +461,20 @@
                 else:
                     out[r, lev, HALF * j : nlon] = (kept - back[j])[:, 0:tail]
 
-        for b in range(2 * blocks):
-            forward(b)
+        @pl.when(sender)
+        def _():
+            landed(halo.at[side, 0], halo_recv.at[side, 0])
+
+        for b in range(blocks):
+            forward((1 - outer) * blocks + b)
+        shifts = between()
+
+        @pl.when(sender)
+        def _():
+            landed(halo.at[side, pl.ds(1, 2)], halo_recv.at[side, 1])
+
+        for b in range(blocks):
+            forward(outer * blocks + b)
         for m in range(RADIX // 2):
             waves = product(ymat[m], (fwd[0, m], fwd[1, m]))
             scaled = jnp.concatenate(
@@ -474,11 +489,7 @@
         for b in range(2 * blocks):
             backward(b)
 
-    @pl.when(position < last)
-    def _():
-        landed(halo.at[1], halo_recv.at[1])
-
-    filter_rows(2)
+    filter_rows(2, 1, lambda: None)
 
     @pl.when(is_first)
     def _():
@@ -493,21 +504,19 @@
             mean_copy(0, mean_in.at[0], root(k)).start()
         mean_copy(0, mean_in.at[0], row(0)).start()
 
-    @pl.when(position > 0)
-    def _():
-        landed(halo.at[0], halo_recv.at[0])
-
-    @pl.when(is_first)
-    def _():
-        landed(mean_in.at[1], mean_recv)
-        own_mean[...] = (mean_in[0] + mean_in[1]) * (1.0 / area)
-
     def mean_columns(value):
         return [jnp.sum(jnp.where(lane == g, value, 0.0), axis=1, keepdims=True) for g in groups]
 
-    columns = mean_columns(own_mean[...])
-    shifts = [jnp.concatenate(columns[2 * b : 2 * b + 2], axis=0) for b in range(blocks)]
-    filter_rows(0, shifts)
+    def known_shifts():
+        @pl.when(is_first)
+        def _():
+            landed(mean_in.at[1], mean_recv)
+            own_mean[...] = (mean_in[0] + mean_in[1]) * (1.0 / area)
+
+        columns = mean_columns(own_mean[...])
+        return [jnp.concatenate(columns[2 * b : 2 * b + 2], axis=0) for b in range(blocks)]
+
+    filter_rows(0, 0, known_shifts)
 
     in_two = jnp.logical_or(is_later_root, jnp.logical_and(y == 0, position > 1))
 
@@ -578,7 +587,7 @@
             vmem((8, HALF), f32), vmem((NX * NC + NY, 8, HALF), f32), vmem((2, 8, HALF), f32),
             vmem((8, HALF), f32),
             vmem((levels // 8, 8, HALF), f32), vmem((levels // 8, 8, HALF), f32),
-            dma((2 * PIECES + 5,)), dma((2,)), dma((2,)), dma, dma, dma, dma, dma, pltpu.SemaphoreType.REGULAR,
+            dma((2 * PIECES + 5,)), dma((2,)), dma((2, 2)), dma, dma, dma, dma, dma, pltpu.SemaphoreType.REGULAR,
         ],
         compiler_params=pltpu.CompilerParams(collective_id=0, has_side_effects=True, vmem_limit_bytes=16 * 2**20),
         name="advect_filter",

time: 25.1 us -> 25.2 us (level)
  no operation moved by 1% of the time
where the time goes in v11:
time: 25.2 us; the launch traced here: 25.1 us
  Pallas kernels  24.2 us (96%)
  local copies, waits for them, and re-layouts  0.88 us (3%)
    pallas_call x1, Pallas kernels, local(): pl.pallas_call(functools.partial(kernel, dims, nlon * cos_sum), out_shape...  24.2 us
    unnamed x1, local copies, waits for them, and re-layouts  0.88 us

profile of v11, /device:TPU:513, one launch (start us, length us, event | category | flops | bytes accessed | tf_op | source)
XLA Modules:
  0.0 25.1 jit_solution(10192521406981655884)
XLA Ops:
  0.0 24.2 %advect_filter.1 = f32[4,32,1440]{2,1,0:T(8,128)S(1)} custom-call(f32[4,32,1440]{2,1,0:T(8,128)} %h_hbm.1, f32[4,32,1440]{2,1,0:T(8,128)} %z_hbm.1, f32[4,32,1440]{2,1,0:T(8,128)} %c_hbm.1, f32[32]{0:T(128)} %rates_hbm.1, f32[32]{0:T(128)} %thr_hbm.1, s32[512]{0:T(512)} %flags_hbm.1, s32[512]{0:T(512)} %cut_hbm.1, f32[1664]{0:T(1024)} %constant.8.clone.scal_hbm, ...), custom_call_target="tpu_custom_call" | custom-call | tf_op jit(solution)/shard_map/advect_filter/pallas_call | solution.py:574
  24.2 0.9 %copy.13 = f32[4,32,1440]{2,1,0:T(8,128)} copy(f32[4,32,1440]{2,1,0:T(8,128)S(1)} %advect_filter.1) | data formatting | bytes 1474560

commit v12 on v9

--- a/solution.py
+++ b/solution.py
@@ -142,7 +142,7 @@
     factor_in = [
         fetch(src, dst, 2 * PIECES + 2 + i) for i, (src, dst) in enumerate(((flags_hbm, flags), (cut_hbm, cut), (ksq_hbm, ksq)))
     ]
-    for copy in small_in + up_in[0] + up_in[1] + [low_rows, c_up]:
+    for copy in small_in + up_in[0] + up_in[1] + [c_up, low_rows]:
         copy.start()
 
     last = total - 1
@@ -251,6 +251,12 @@
     wide, rest = [0.0 for g in groups], [0.0 for g in groups]
     for r in order:
         if r == 0:
+            c_up.wait()
+
+            @pl.when(core == 0)
+            def _():
+                halo_copy(0, 2).start()
+
             low_rows.wait()
         for g in groups:
             lev = pl.ds(8 * g, 8)
@@ -294,16 +300,10 @@
     def _():
         send_b(row(1))
 
-    c_up.wait()
-
     @pl.when(jnp.logical_and(core != 0, position < last))
     def _():
-        halo_copy(0, 0).start()
-        halo_copy(0, 1).start()
-
-    @pl.when(position < last)
-    def _():
-        halo_copy(0, 2).start()
+        for field in range(3):
+            halo_copy(0, field).start()
 
     @pl.when(position == 0)
     def _():
@@ -420,7 +420,7 @@
         second = jnp.dot(hilo[0:units], table[1], preferred_element_type=jnp.float32)
         return first_part[0:units] + first_part[units : 2 * units] + second
 
-    def filter_rows(row0, shifts=None):
+    def filter_rows(row0, known=None):
         def block_of(b):
             return row0 + b // blocks, pl.ds(16 * (b % blocks), 16), pl.ds(16 * b, 16), pl.ds(units + 16 * b, 16)
 
@@ -460,6 +460,7 @@
 
         for b in range(2 * blocks):
             forward(b)
+        shifts = known() if known else None
         for m in range(RADIX // 2):
             waves = product(ymat[m], (fwd[0, m], fwd[1, m]))
             scaled = jnp.concatenate(
@@ -497,17 +498,19 @@
     def _():
         landed(halo.at[0], halo_recv.at[0])
 
-    @pl.when(is_first)
-    def _():
-        landed(mean_in.at[1], mean_recv)
-        own_mean[...] = (mean_in[0] + mean_in[1]) * (1.0 / area)
-
     def mean_columns(value):
         return [jnp.sum(jnp.where(lane == g, value, 0.0), axis=1, keepdims=True) for g in groups]
 
-    columns = mean_columns(own_mean[...])
-    shifts = [jnp.concatenate(columns[2 * b : 2 * b + 2], axis=0) for b in range(blocks)]
-    filter_rows(0, shifts)
+    def known_shifts():
+        @pl.when(is_first)
+        def _():
+            landed(mean_in.at[1], mean_recv)
+            own_mean[...] = (mean_in[0] + mean_in[1]) * (1.0 / area)
+
+        columns = mean_columns(own_mean[...])
+        return [jnp.concatenate(columns[2 * b : 2 * b + 2], axis=0) for b in range(blocks)]
+
+    filter_rows(0, known_shifts)
 
     in_two = jnp.logical_or(is_later_root, jnp.logical_and(y == 0, position > 1))
 

time: 25.1 us -> 25.2 us (level)
  no operation moved by 1% of the time
where the time goes in v12:
time: 25.2 us; the launch traced here: 25 us
  Pallas kernels  24.1 us (96%)
  local copies, waits for them, and re-layouts  0.88 us (3%)
    pallas_call x1, Pallas kernels, local(): pl.pallas_call(functools.partial(kernel, dims, nlon * cos_sum), out_shape...  24.1 us
    unnamed x1, local copies, waits for them, and re-layouts  0.88 us

profile of v12, /device:TPU:513, one launch (start us, length us, event | category | flops | bytes accessed | tf_op | source)
XLA Modules:
  0.0 25.0 jit_solution(7346160490447259371)
XLA Ops:
  0.0 24.1 %advect_filter.1 = f32[4,32,1440]{2,1,0:T(8,128)S(1)} custom-call(f32[4,32,1440]{2,1,0:T(8,128)} %h_hbm.1, f32[4,32,1440]{2,1,0:T(8,128)} %z_hbm.1, f32[4,32,1440]{2,1,0:T(8,128)} %c_hbm.1, f32[32]{0:T(128)} %rates_hbm.1, f32[32]{0:T(128)} %thr_hbm.1, s32[512]{0:T(512)} %flags_hbm.1, s32[512]{0:T(512)} %cut_hbm.1, f32[1664]{0:T(1024)} %constant.8.clone.scal_hbm, ...), custom_call_target="tpu_custom_call" | custom-call | tf_op jit(solution)/shard_map/advect_filter/pallas_call | solution.py:568
  24.2 0.9 %copy.13 = f32[4,32,1440]{2,1,0:T(8,128)} copy(f32[4,32,1440]{2,1,0:T(8,128)S(1)} %advect_filter.1) | data formatting | bytes 1474560

commit v13 on v9

--- a/solution.py
+++ b/solution.py
@@ -13,6 +13,7 @@
 MESH = pl.DeviceIdType.MESH
 NX, NY, NC = 8, 8, 2
 PIECES = 2
+NEAR_ROOTS = (1, 2)
 RADIX = 12
 HALF = 128
 ROOT = math.sqrt(0.75)
@@ -490,8 +491,8 @@
         for k in range(1, NY):
             for member in members[2 * k - 2 : 2 * k]:
                 mean_copy(0, mean_in.at[0], row(member)).start()
-            mean_copy(0, mean_in.at[0], root(k)).start()
-        mean_copy(0, mean_in.at[0], row(0)).start()
+            if k in NEAR_ROOTS:
+                mean_copy(0, mean_in.at[0], root(k)).start()
 
     @pl.when(position > 0)
     def _():
@@ -508,6 +509,13 @@
     columns = mean_columns(own_mean[...])
     shifts = [jnp.concatenate(columns[2 * b : 2 * b + 2], axis=0) for b in range(blocks)]
     filter_rows(0, shifts)
+
+    @pl.when(is_first)
+    def _():
+        for k in range(1, NY):
+            if k not in NEAR_ROOTS:
+                mean_copy(0, mean_in.at[0], root(k)).start()
+        mean_copy(0, mean_in.at[0], row(0)).start()
 
     in_two = jnp.logical_or(is_later_root, jnp.logical_and(y == 0, position > 1))
 

time: 25.1 us -> 26 us (1.036)
  Pallas kernels: 24.1 us -> 25 us
    pallas_call x1, Pallas kernels: 24.1 us -> 25 us  [local(): pl.pallas_call(functools.partial(kernel, dims, nlon * cos_sum), out_shape...]
where the time goes in v13:
time: 26 us; the launch traced here: 25.9 us
  Pallas kernels  25 us (96%)
  local copies, waits for them, and re-layouts  0.88 us (3%)
    pallas_call x1, Pallas kernels, local(): pl.pallas_call(functools.partial(kernel, dims, nlon * cos_sum), out_shape...  25 us
    unnamed x1, local copies, waits for them, and re-layouts  0.88 us

profile of v13, /device:TPU:513, one launch (start us, length us, event | category | flops | bytes accessed | tf_op | source)
XLA Modules:
  0.0 25.9 jit_solution(5043260049527007729)
XLA Ops:
  0.0 25.0 %advect_filter.1 = f32[4,32,1440]{2,1,0:T(8,128)S(1)} custom-call(f32[4,32,1440]{2,1,0:T(8,128)} %h_hbm.1, f32[4,32,1440]{2,1,0:T(8,128)} %z_hbm.1, f32[4,32,1440]{2,1,0:T(8,128)} %c_hbm.1, f32[32]{0:T(128)} %rates_hbm.1, f32[32]{0:T(128)} %thr_hbm.1, s32[512]{0:T(512)} %flags_hbm.1, s32[512]{0:T(512)} %cut_hbm.1, f32[1664]{0:T(1024)} %constant.8.clone.scal_hbm, ...), custom_call_target="tpu_custom_call" | custom-call | tf_op jit(solution)/shard_map/advect_filter/pallas_call | solution.py:573
  25.0 0.9 %copy.13 = f32[4,32,1440]{2,1,0:T(8,128)} copy(f32[4,32,1440]{2,1,0:T(8,128)S(1)} %advect_filter.1) | data formatting | bytes 1474560

commit v14 on v9

--- a/solution.py
+++ b/solution.py
@@ -142,7 +142,7 @@
     factor_in = [
         fetch(src, dst, 2 * PIECES + 2 + i) for i, (src, dst) in enumerate(((flags_hbm, flags), (cut_hbm, cut), (ksq_hbm, ksq)))
     ]
-    for copy in small_in + up_in[0] + up_in[1] + [low_rows, c_up]:
+    for copy in up_in[0] + up_in[1] + small_in + [low_rows, c_up]:
         copy.start()
 
     last = total - 1

time: 25.1 us -> 25.1 us (level)
  no operation moved by 1% of the time
where the time goes in v14:
time: 25.1 us; the launch traced here: 25 us
  Pallas kernels  24.1 us (96%)
  local copies, waits for them, and re-layouts  0.88 us (4%)
    pallas_call x1, Pallas kernels, local(): pl.pallas_call(functools.partial(kernel, dims, nlon * cos_sum), out_shape...  24.1 us
    unnamed x1, local copies, waits for them, and re-layouts  0.88 us

profile of v14, /device:TPU:513, one launch (start us, length us, event | category | flops | bytes accessed | tf_op | source)
XLA Modules:
  0.0 25.0 jit_solution(6448770432304611734)
XLA Ops:
  0.0 24.1 %advect_filter.1 = f32[4,32,1440]{2,1,0:T(8,128)S(1)} custom-call(f32[4,32,1440]{2,1,0:T(8,128)} %h_hbm.1, f32[4,32,1440]{2,1,0:T(8,128)} %z_hbm.1, f32[4,32,1440]{2,1,0:T(8,128)} %c_hbm.1, f32[32]{0:T(128)} %rates_hbm.1, f32[32]{0:T(128)} %thr_hbm.1, s32[512]{0:T(512)} %flags_hbm.1, s32[512]{0:T(512)} %cut_hbm.1, f32[1664]{0:T(1024)} %constant.8.clone.scal_hbm, ...), custom_call_target="tpu_custom_call" | custom-call | tf_op jit(solution)/shard_map/advect_filter/pallas_call | solution.py:565
  24.1 0.9 %copy.13 = f32[4,32,1440]{2,1,0:T(8,128)} copy(f32[4,32,1440]{2,1,0:T(8,128)S(1)} %advect_filter.1) | data formatting | bytes 1474560

commit v15 on v9

--- a/solution.py
+++ b/solution.py
@@ -12,7 +12,7 @@
 
 MESH = pl.DeviceIdType.MESH
 NX, NY, NC = 8, 8, 2
-PIECES = 2
+PIECES = 4
 RADIX = 12
 HALF = 128
 ROOT = math.sqrt(0.75)

time: 25.1 us -> 25.1 us (level)
  no operation moved by 1% of the time
where the time goes in v15:
time: 25.1 us; the launch traced here: 25 us
  Pallas kernels  24.1 us (96%)
  local copies, waits for them, and re-layouts  0.88 us (4%)
    pallas_call x1, Pallas kernels, local(): pl.pallas_call(functools.partial(kernel, dims, nlon * cos_sum), out_shape...  24.1 us
    unnamed x1, local copies, waits for them, and re-layouts  0.88 us

profile of v15, /device:TPU:513, one launch (start us, length us, event | category | flops | bytes accessed | tf_op | source)
XLA Modules:
  0.0 25.0 jit_solution(13033165201931149071)
XLA Ops:
  0.0 24.1 %advect_filter.1 = f32[4,32,1440]{2,1,0:T(8,128)S(1)} custom-call(f32[4,32,1440]{2,1,0:T(8,128)} %h_hbm.1, f32[4,32,1440]{2,1,0:T(8,128)} %z_hbm.1, f32[4,32,1440]{2,1,0:T(8,128)} %c_hbm.1, f32[32]{0:T(128)} %rates_hbm.1, f32[32]{0:T(128)} %thr_hbm.1, s32[512]{0:T(512)} %flags_hbm.1, s32[512]{0:T(512)} %cut_hbm.1, f32[1664]{0:T(1024)} %constant.8.clone.scal_hbm, ...), custom_call_target="tpu_custom_call" | custom-call | tf_op jit(solution)/shard_map/advect_filter/pallas_call | solution.py:565
  24.1 0.9 %copy.13 = f32[4,32,1440]{2,1,0:T(8,128)} copy(f32[4,32,1440]{2,1,0:T(8,128)S(1)} %advect_filter.1) | data formatting | bytes 1474560
